TPU v7x, 512 devices: a whole 4x8x8 slice. The times are simulated.
512 devices in a mesh: grp: 8 (over z), tp: 16 (over x_lo, y), src: 4 (over x_hi, core).
Axes of the slice: x: 4 (x_hi: 2, x_lo: 2; x = x_hi * 2 + x_lo), y: 8, z: 8, core: 2. Of those that a mesh axis runs over, the one named last changes fastest.
Arguments:
- hidden_in: bfloat16 [2048, 5120], P(('grp', 'src')), may hold values from -6 to 6
- attn_gain: float32 [5120], replicated, may hold values from 0.5 to 1.5
- w_qkv: int32 [1280, 5120], P(None, 'tp'), may hold values from -2147483648 to 2147483646
- qkv_scale: float32 [5120], P('tp'), may hold values from 0.0001118034 to 0.00041926274
- q_gain: float32 [128], replicated, may hold values from 0.25 to 1.75
- k_gain: float32 [128], replicated, may hold values from 0.1 to 1.9
- key_cache: bfloat16 [32, 64, 128, 512], P(('grp', 'src'), 'tp'), may hold values from -400 to 400
- value_cache: bfloat16 [32, 64, 128, 512], P(('grp', 'src'), 'tp'), may hold values from -9 to 9
- lengths: int32 [32, 64], P(('grp', 'src'), 'tp'), may hold values from 1 to 128, as said below
- w_out: int32 [1024, 5120], P('tp'), may hold values from -2147483648 to 2147483646
- out_scale: float32 [5120], replicated, may hold values from 0.0003125 to 0.00125
- mlp_gain: float32 [5120], replicated, may hold values from 0.5 to 1.5
- w_gate: int32 [1280, 12800], P(('grp', 'src'), 'tp'), may hold values from -2147483648 to 2147483646
- w_up: int32 [1280, 12800], P(('grp', 'src'), 'tp'), may hold values from -2147483648 to 2147483646
- gate_scale: float32 [12800], P('tp'), may hold values from 0.0001118034 to 0.00041926274
- up_scale: float32 [12800], P('tp'), may hold values from 0.0001118034 to 0.00041926274
- w_down: int32 [3200, 5120], P('tp', ('grp', 'src')), may hold values from -2147483648 to 2147483646
- down_scale: float32 [5120], replicated, may hold values from 0.00013258251 to 0.00053033006
Outputs:
- layer_out: bfloat16 [2048, 5120], P(('grp', 'src'), 'tp')
Inputs may be any that keep to these rules, and one draw needn't show every extreme that they name: `lengths`: some sequence has exactly 128 cached positions.
All inputs are finite; a program needn't handle non-finite values.
Results may differ from a plain program's by a relative error of at most 0.028.
Values may be sent and summed in bfloat16 or wider, within the bound.
A program may use at most 64 MiB of HBM per device.

v0:
```python
import math

import jax
import jax.numpy as jnp
from jax import lax
from jax.experimental import pallas as pl
from jax.experimental.pallas import tpu as pltpu
from jax.sharding import PartitionSpec as P

D = 5120
HALF = 2560
HEADS = 32
KV = 4
HEAD = 128
ROWS = 64
ALL = 256
YS = 8
ZS = 8
HID = 200
PAD = 256
EPS = 1e-06
ROPE = 1000000.0
MESH = pl.DeviceIdType.MESH
F32 = jnp.float32
BF = jnp.bfloat16
NEAR = (0, 1, 7, 2, 6, 3, 5, 4)


def mo(value, k):
    return pl.multiple_of(value, k)


def byte_of(words, k):
    return jnp.right_shift(jnp.left_shift(words, 24 - 8 * k), 24).astype(F32).astype(BF)


def one_hot(n, used, group, stride):
    row = lax.broadcasted_iota(jnp.int32, (n, n), 0)
    col = lax.broadcasted_iota(jnp.int32, (n, n), 1)
    shift = stride.bit_length() - 1
    k, r = jnp.right_shift(col, shift), jnp.bitwise_and(col, stride - 1)
    return jnp.where((row == 4 * r + k) & (r < used), 1.0, 0.0).astype(BF)


def dot(a, b):
    return jnp.dot(a, b, preferred_element_type=F32)


def kernel(
    hid, again, wq, qscale, gains, kc, vc, ctab, stab, ltab, wout, oscale, mgain, gu4, gsc, dn4, dscale,
    out,
    stage, bsend, brecv, qs, vs, hsend, hrecv, wo_r, wo, pm, rs, X, xk, gub, dnp, dnb, wg, wd, pd, sib,
    pre, spre, splain, smerge, rplain, rmerge, u, yr,
    w1s, w1r, wos, wor, zs, zr, bs, br, hs, hr, rss, rsr, fys, fyr, fxs, fxr, fqs, fqr, fss, fsr,
    sbs, sbr, xps, xpr, xms, xmr, yss, ysr,
):
    z = lax.axis_index("grp")
    tp = lax.axis_index("tp")
    src = lax.axis_index("src")
    xl, y = tp // YS, tp % YS
    xh, core = src // 2, src % 2
    x = xh * 2 + xl

    def at_x(xx, cc):
        return {"tp": (xx % 2) * YS + y, "src": (xx // 2) * 2 + cc}

    xp, xm, xo = (x + 1) % 4, (x + 3) % 4, (x + 2) % 4
    PLUS, MINUS = at_x(xp, core), at_x(xm, core)
    SIB = {"src": xh * 2 + 1 - core}
    ZP, ZM = {"grp": (z + 1) % ZS}, {"grp": (z + ZS - 1) % ZS}

    def rcopy(a, b, s, r, to):
        return pltpu.make_async_remote_copy(
            src_ref=a, dst_ref=b, send_sem=s, recv_sem=r, device_id=to, device_id_type=MESH
        )

    barrier = pltpu.get_barrier_semaphore()

    def greet_tp(d, _):
        pl.semaphore_signal(barrier, inc=1, device_id={"tp": (tp + d) % 16}, device_id_type=MESH)
        return 0

    def greet_src(d, _):
        pl.semaphore_signal(barrier, inc=1, device_id={"src": (src + d) % 4}, device_id_type=MESH)
        return 0

    lax.fori_loop(1, 16, greet_tp, 0)
    lax.fori_loop(1, 4, greet_src, 0)
    across = {"tp": (1 - xl) * YS + y, "src": (1 - xh) * 2 + core}
    for to in (across, ZP, ZM):
        pl.semaphore_signal(barrier, inc=1, device_id=to, device_id_type=MESH)
    pl.semaphore_wait(barrier, 21)

    def w1_gu(d):
        s2 = (src + d) % 4
        return rcopy(
            gu4.at[s2], gub.at[0, pl.ds(mo(src * 40, 8), 40), :], w1s.at[0, d], w1r.at[0, src], {"src": s2}
        )

    def w1_dn(d):
        s2 = (src + d) % 4
        return rcopy(dn4.at[s2], dnp.at[src], w1s.at[1, d], w1r.at[1, src], {"src": s2})

    for d in (2, 3, 1):
        w1_gu(d).start()
        w1_dn(d).start()
    wo_side = (x + 1 + 2 * core) % 4
    wo_copy = rcopy(
        wout.at[:, pl.ds(mo((1 - xl) * HALF, 128), HALF)], wo_r, wos, wor, at_x(wo_side, core)
    )
    wo_copy.start()
    gub[0, pl.ds(mo(src * 40, 8), 40), :] = gu4[src]
    dnp[src] = dn4[src]

    total = jnp.zeros((ROWS, 1), F32)
    for g in range(10):
        v = hid[:, g * 512 : (g + 1) * 512].astype(F32)
        total = total + jnp.sum(v * v, axis=1, keepdims=True)
    rms = lax.rsqrt(total * (1.0 / D) + EPS)
    P512 = one_hot(512, 128, 4, 128)
    stage[...] = jnp.broadcast_to(rms, (ROWS, 384))

    def qkv_group(g, acc):
        at = pl.ds(mo(g * 512, 512), 512)
        r = stage[:, 0:1]
        v = (hid[:, at].astype(F32) * r * again[:, at]).astype(BF)
        v = dot(v, P512).astype(BF)
        w = wq[pl.ds(mo(g * 128, 128), 128), :]
        for k in range(4):
            acc = acc + dot(v[:, k * 128 : (k + 1) * 128], byte_of(w, k))
        return acc

    acc = lax.fori_loop(0, 10, qkv_group, jnp.zeros((ROWS, 320), F32))
    qkv = (acc * qscale[...]).astype(BF).astype(F32)
    stage[...] = jnp.zeros((ROWS, 384), F32)
    stage[:, :320] = qkv
    odd_y = (y % 2) == 1
    placed = stage[...]
    placed = jnp.where(odd_y, pltpu.roll(placed, 64, 1), placed)
    for t in range(16):
        bsend[t] = placed[4 * t : 4 * t + 4, :]

    def b_copy(d):
        to = (tp + d) % 16
        return rcopy(bsend.at[to], brecv.at[tp], bs.at[to], br.at[tp], {"tp": to})

    def b_in(d):
        frm = (tp + d) % 16
        return rcopy(bsend.at[frm], brecv.at[frm], bs.at[frm], br.at[frm], {"tp": frm})

    def start_b(d, _):
        b_copy(d).start()
        return 0

    def wait_b(d, _):
        b_in(d).wait_recv()
        return 0

    lax.fori_loop(1, 16, start_b, 0)
    brecv[pl.ds(tp, 1)] = bsend[pl.ds(tp, 1)]

    def w1_in(j, d):
        s2 = (src + d) % 4
        if j == 0:
            return rcopy(gu4.at[s2], gub.at[0, pl.ds(mo(s2 * 40, 8), 40), :], w1s.at[0, d], w1r.at[0, s2], {"src": s2})
        return rcopy(dn4.at[s2], dnp.at[s2], w1s.at[1, d], w1r.at[1, s2], {"src": s2})

    for d in (1, 2, 3):
        w1_in(0, d).wait_recv()
        w1_in(1, d).wait_recv()
    dnb[0] = jnp.concatenate([dnp[0], dnp[1], dnp[2], dnp[3]], axis=1)

    def ring(step, way):
        a = step - 1 if way == 0 else (9 - step) % 8
        b = step if way == 0 else 8 - step
        to = ZP if way == 0 else ZM
        if step == 4:
            g_at, d_at = (slice(0, 80), slice(0, 32)) if way == 0 else (slice(80, 160), slice(32, 56))
        else:
            g_at, d_at = slice(0, 160), slice(0, 56)
        one = rcopy(gub.at[a, g_at, :], gub.at[b, g_at, :], zs.at[way, step - 1, 0], zr.at[way, step - 1, 0], to)
        two = rcopy(dnb.at[a, d_at, :], dnb.at[b, d_at, :], zs.at[way, step - 1, 1], zr.at[way, step - 1, 1], to)
        return one, two

    def ring_start(step):
        for way in (0, 1):
            for c in ring(step, way):
                c.start()

    def ring_wait(step):
        for way in (0, 1):
            for c in ring(step, way):
                c.wait_recv()

    def unpack(slot):
        zz = (z + ZS - slot) % ZS

        def rows(i, _):
            w = gub[slot, pl.ds(mo(i * 32, 32), 32), :]
            for k in range(4):
                wg[k, pl.ds(mo(zz * 160 + i * 32, 32), 32), :] = byte_of(w, k)
            return 0

        lax.fori_loop(0, 5, rows, 0)
        w = dnb[slot]
        for k in range(4):
            wd[k * 64 : k * 64 + 56, pl.ds(mo(zz * 640, 128), 640)] = byte_of(w, k)

    ring_start(1)
    wd[...] = jnp.zeros(wd.shape, BF)
    unpack(0)
    own_words = wout.at[:, pl.ds(mo(xl * HALF, 128), HALF)]

    def unpack_wo(ref, base):
        def cols(i, _):
            at = pl.ds(mo(i * 640, 128), 640)
            for hl in range(2):
                w = ref[hl * 32 : hl * 32 + 32, at]
                for k in range(4):
                    wo[pl.ds(mo(base + hl * 128 + k * 32, 32), 32), at] = byte_of(w, k)
            return 0

        lax.fori_loop(0, 4, cols, 0)

    unpack_wo(own_words, xl * 256)

    lax.fori_loop(1, 16, wait_b, 0)
    lane = lax.broadcasted_iota(jnp.int32, (4, HEAD), 1)
    for p in range(8):
        even, odd = brecv[2 * p], brecv[2 * p + 1]
        pieces = (
            even[:, 0:128],
            even[:, 128:256],
            jnp.where(lane < 64, even[:, 256:384], odd[:, 0:128]),
            odd[:, 128:256],
            odd[:, 256:384],
        )
        for j, piece in enumerate(pieces):
            h = 5 * p + j
            if h < HEADS:
                qs[4 * h : 4 * h + 4, :] = piece
            elif h < HEADS + KV:
                at = 128 + 8 * (h - HEADS)
                qs[at : at + 4, :] = piece
                qs[at + 4 : at + 8, :] = piece
            else:
                at = 8 * (h - HEADS - KV)
                vs[at : at + 4, :] = piece
                vs[at + 4 : at + 8, :] = piece
    v = qs[...]
    v = v * lax.rsqrt(jnp.mean(v * v, axis=1, keepdims=True) + EPS)
    row = lax.broadcasted_iota(jnp.int32, (160, HEAD), 0)
    v = v * jnp.where(row < 128, gains[0:1, :], gains[1:2, :])
    turned = pltpu.roll(v, 64, 1)
    v = v.reshape(20, 8, HEAD) * ctab[...][None] + turned.reshape(20, 8, HEAD) * stab[...][None]
    v = v.reshape(160, HEAD).astype(BF)
    scale = 1.0 / math.sqrt(HEAD)
    seq = jnp.bitwise_and(lax.broadcasted_iota(jnp.int32, (32, HEAD), 0), 3)
    place = lax.broadcasted_iota(jnp.int32, (8, HEAD), 1)
    live = jnp.where(place < ltab[...], 1.0, 0.0)
    live = jnp.broadcast_to(live[None], (4, 8, HEAD)).reshape(32, HEAD) > 0.5
    heads = []
    for g in range(KV):
        q = v[32 * g : 32 * g + 32]
        newk = v[128 + 8 * g : 136 + 8 * g].astype(F32)
        own = jnp.sum((q.astype(F32).reshape(4, 8, HEAD) * newk[None]).reshape(32, HEAD), axis=1, keepdims=True)
        own = own * scale
        s = jnp.zeros((32, HEAD), F32)
        for b in range(4):
            sb = lax.dot_general(
                q, kc[b, :, g * 128 : (g + 1) * 128], (((1,), (1,)), ((), ())), preferred_element_type=F32
            )
            s = jnp.where(seq == b, sb, s)
        s = jnp.where(live, s * scale, -jnp.inf)
        top = jnp.maximum(jnp.max(s, axis=1, keepdims=True), own)
        e = jnp.exp(s - top)
        own_e = jnp.exp(own - top)
        den = jnp.sum(e, axis=1, keepdims=True) + own_e
        newv = vs[8 * g : 8 * g + 8, :]
        low = own_e.astype(BF).astype(F32)
        num = (low.reshape(4, 8, 1) * newv[None]).reshape(32, HEAD)
        for b in range(4):
            eb = jnp.where(seq == b, e, 0.0).astype(BF)
            num = num + dot(eb, vc[b, :, g * 128 : (g + 1) * 128])
        heads.append(num / den)
    for yy in range(YS):
        g, at = yy // 4, 8 * (yy % 4)
        hsend[yy] = jnp.concatenate([heads[g][at : at + 8], heads[g + 2][at : at + 8]], axis=0).astype(BF)

    def h_slot(t):
        return hrecv.at[pl.ds(mo(t * 16, 16), 16), :]

    def h_copy(d):
        to = (tp + d) % 16
        return rcopy(hsend.at[to % YS], h_slot(tp), hs.at[to], hr.at[tp], {"tp": to})

    def start_h(d, _):
        h_copy(d).start()
        return 0

    def wait_h(d, _):
        frm = (tp + d) % 16
        rcopy(hsend.at[frm % YS], h_slot(frm), hs.at[frm], hr.at[frm], {"tp": frm}).wait_recv()
        return 0

    lax.fori_loop(1, 16, start_h, 0)
    hrecv[pl.ds(mo(tp * 16, 16), 16), :] = hsend[y]

    wo_copy.wait_recv()
    unpack_wo(wo_r, (1 - xl) * 256)

    lax.fori_loop(1, 16, wait_h, 0)
    P128 = one_hot(128, 32, 4, 32)
    got = hrecv[...]
    t = lax.broadcasted_iota(jnp.int32, (ROWS, 256), 0)
    c = lax.broadcasted_iota(jnp.int32, (ROWS, 256), 1)
    zcat = []
    for hl in range(4):
        want = jnp.right_shift(t, 2) * 16 + hl * 4 + jnp.bitwise_and(t, 3)
        pick = jnp.where(c == want, 1.0, 0.0).astype(BF)
        zcat.append(dot(dot(pick, got).astype(BF), P128).astype(BF))
    zcat = jnp.concatenate(zcat, axis=1)

    def part(yy):
        return pl.ds(mo(32 * (yy // 4), 32), 32), pl.ds(mo(640 * (yy % 4), 128), 640)

    for cb in range(4):
        pm[:, cb * 640 : cb * 640 + 640] = dot(zcat, wo[:, cb * 640 : cb * 640 + 640]).astype(BF)

    def r_copy(d):
        to = (y + d) % YS
        a, b = part(to)
        return rcopy(pm.at[a, b], rs.at[y], rss.at[to], rsr.at[y], {"tp": xl * YS + to})

    def start_r(d, _):
        r_copy(d).start()
        return 0

    def wait_r(d, _):
        frm = (y + d) % YS
        a, b = part(frm)
        rcopy(pm.at[a, b], rs.at[frm], rss.at[frm], rsr.at[frm], {"tp": xl * YS + frm}).wait_recv()
        return 0

    lax.fori_loop(1, YS, start_r, 0)
    a, b = part(y)
    rs[y] = pm[a, b]

    ring_wait(1)
    ring_start(2)
    unpack(1)
    unpack(7)

    lax.fori_loop(1, YS, wait_r, 0)
    mid = rs[0].astype(F32)
    for i in range(1, YS):
        mid = mid + rs[i].astype(F32)
    col0 = mo(xl * HALF + 640 * (y % 4), 128)
    mid = hid[a, pl.ds(col0, 640)].astype(F32) + mid * oscale[:, pl.ds(col0, 640)]
    X[pl.ds(mo(src * 64 + 32 * (y // 4), 32), 32), pl.ds(col0, 640)] = mid.astype(BF)

    def blk(xx, cc, yy):
        r0 = ((xx // 2) * 2 + cc) * 64 + 32 * (yy // 4)
        c0 = (xx % 2) * HALF + 640 * (yy % 4)
        return X.at[pl.ds(mo(r0, 32), 32), pl.ds(mo(c0, 128), 640)]

    def fy_copy(d):
        to = (y + d) % YS
        return rcopy(blk(x, core, y), blk(x, core, y), fys.at[to], fyr.at[y], {"tp": xl * YS + to})

    for d in NEAR[1:]:
        fy_copy(d).start()

    def fx_copy(way, i):
        b0 = blk(x, core, (y + i) % YS)
        return rcopy(b0, b0, fxs.at[way, i], fxr.at[way, i], PLUS if way == 0 else MINUS)

    def fx_in(way, i):
        b0 = blk(xm if way == 0 else xp, core, (y + i) % YS)
        return rcopy(b0, b0, fxs.at[way, i], fxr.at[way, i], MINUS if way == 0 else PLUS)

    def fq_copy(i):
        way = i % 2
        b0 = blk(xm if way == 0 else xp, core, (y + i) % YS)
        return rcopy(b0, b0, fqs.at[i], fqr.at[i], PLUS if way == 0 else MINUS)

    def fq_in(i):
        b0 = blk(xo, core, (y + i) % YS)
        return rcopy(b0, b0, fqs.at[i], fqr.at[i], MINUS if i % 2 == 0 else PLUS)

    froms = (x, xm, xp, xo)

    def fs_copy(j, i):
        b0 = blk(froms[j], core, (y + i) % YS)
        return rcopy(b0, b0, fss.at[j, i], fsr.at[j, i], SIB)

    def fs_in(j, i):
        b0 = blk(froms[j], 1 - core, (y + i) % YS)
        return rcopy(b0, b0, fss.at[j, i], fsr.at[j, i], SIB)

    for i in NEAR:
        yy = (y + i) % YS
        if i:
            b0 = blk(x, core, yy)
            rcopy(b0, b0, fys.at[yy], fyr.at[yy], {"tp": xl * YS + yy}).wait_recv()
        fx_copy(0, i).start()
        fx_copy(1, i).start()
        fs_copy(0, i).start()
    ring_wait(2)
    ring_start(3)
    for i in NEAR:
        fx_in(0, i).wait_recv()
        fx_in(1, i).wait_recv()
        fq_copy(i).start()
        fs_copy(1, i).start()
        fs_copy(2, i).start()
    unpack(2)
    unpack(6)
    ring_wait(3)
    ring_start(4)
    unpack(3)
    unpack(5)
    for i in NEAR:
        fq_in(i).wait_recv()
        fs_copy(3, i).start()
    for j in range(4):
        for i in NEAR:
            fs_in(j, i).wait_recv()

    P512 = one_hot(512, 128, 4, 128)

    def norm_rows(m, _):
        at = pl.ds(mo(m * 64, 64), 64)
        total = jnp.zeros((64, 1), F32)
        for g in range(10):
            v = X[at, g * 512 : (g + 1) * 512].astype(F32)
            total = total + jnp.sum(v * v, axis=1, keepdims=True)
        rms = lax.rsqrt(total * (1.0 / D) + EPS)
        for g in range(10):
            v = X[at, g * 512 : (g + 1) * 512].astype(F32)
            v = (v * rms * mgain[:, g * 512 : (g + 1) * 512]).astype(BF)
            v = dot(v, P512).astype(BF)
            for k in range(4):
                xk[k, at, g * 128 : (g + 1) * 128] = v[:, k * 128 : (k + 1) * 128]
        return 0

    lax.fori_loop(0, 4, norm_rows, 0)
    ring_wait(4)
    unpack(4)
    both = dot(xk[0], wg[0])
    for k in range(1, 4):
        both = both + dot(xk[k], wg[k])
    both = both * gsc[pl.ds(src, 1), :]
    gate, up = both[:, :PAD], both[:, PAD:]
    act = (gate / (1.0 + jnp.exp(-gate)) * up).astype(BF)
    act = dot(act, one_hot(PAD, HID // 4, 4, 64)).astype(BF)
    xk[0, :, :PAD] = act

    def down(n, _):
        at = pl.ds(mo(n * 640, 128), 640)
        pd[:, at] = dot(xk[0, :, :PAD], wd[:, at]).astype(BF)
        return 0

    lax.fori_loop(0, 8, down, 0)

    def slab_rows(h, cc):
        return pl.ds(mo((h * 2 + cc) * 64, 64), 64)

    def sb_copy(h):
        return rcopy(pd.at[slab_rows(h, 1 - core), :], sib.at[h], sbs.at[h], sbr.at[h], SIB)

    for h in (0, 1):
        sb_copy(h).start()
    for h in (0, 1):
        sb_copy(h).wait_recv()

    def slab(xx, half):
        at = pl.ds(mo((xx % 2) * HALF + half * 1280, 128), 1280)
        return pd[slab_rows(xx // 2, core), at].astype(F32) + sib[xx // 2, :, at].astype(F32)

    sides = (PLUS, MINUS)
    nexts = (xp, xm)
    pre_copies = [rcopy(spre.at[w], pre.at[w], xps.at[w], xpr.at[w], sides[w]) for w in (0, 1)]
    plain = [rcopy(splain.at[w], rplain.at[w], xms.at[w, 0], xmr.at[w, 0], sides[w]) for w in (0, 1)]
    merge = [rcopy(smerge.at[w], rmerge.at[w], xms.at[w, 1], xmr.at[w, 1], sides[w]) for w in (0, 1)]
    for w in (0, 1):
        spre[w] = slab(xo, w).astype(BF)
        pre_copies[w].start()
    for w in (0, 1):
        splain[w] = slab(nexts[w], 1 - w).astype(BF)
        plain[w].start()
    for w in (0, 1):
        pre_copies[w].wait_recv()
        smerge[w] = (slab(nexts[w], w) + pre[w].astype(F32)).astype(BF)
        merge[w].start()
    mine = [slab(x, 0), slab(x, 1)]
    for w in (0, 1):
        plain[w].wait_recv()
        mine[1 - w] = mine[1 - w] + rplain[w].astype(F32)
    for w in (0, 1):
        merge[w].wait_recv()
        mine[w] = mine[w] + rmerge[w].astype(F32)
    u[:, :1280] = mine[0].astype(BF)
    u[:, 1280:] = mine[1].astype(BF)

    def window(yy):
        return pl.ds(mo(320 * yy - 64 * (yy % 2), 128), 384)

    def y_copy(d):
        to = (y + d) % YS
        return rcopy(u.at[:, window(to)], yr.at[y], yss.at[to], ysr.at[y], {"tp": xl * YS + to})

    def y_in(d):
        frm = (y + d) % YS
        return rcopy(u.at[:, window(frm)], yr.at[frm], yss.at[frm], ysr.at[frm], {"tp": xl * YS + frm})

    for d in NEAR[1:]:
        y_copy(d).start()
    yr[y] = u[:, window(y)]
    for d in NEAR[1:]:
        y_in(d).wait_recv()
    last = yr[0].astype(F32)
    for i in range(1, YS):
        last = last + yr[i].astype(F32)
    at = pl.ds(mo(xl * HALF + 320 * y - 64 * (y % 2), 128), 384)
    last = X[pl.ds(mo(src * 64, 64), 64), at].astype(F32) + last * dscale[:, at]
    last = jnp.where(odd_y, pltpu.roll(last, 320, 1), last)
    out[...] = last[:, :320].astype(BF)

    for d in (1, 2, 3):
        w1_gu(d).wait_send()
        w1_dn(d).wait_send()
    wo_copy.wait_send()
    for step in (1, 2, 3, 4):
        for way in (0, 1):
            for c in ring(step, way):
                c.wait_send()

    def sent_tp(d, _):
        b_copy(d).wait_send()
        h_copy(d).wait_send()
        return 0

    def sent_y(d, _):
        r_copy(d).wait_send()
        fy_copy(d).wait_send()
        y_copy(d).wait_send()
        return 0

    lax.fori_loop(1, 16, sent_tp, 0)
    lax.fori_loop(1, YS, sent_y, 0)
    for i in range(YS):
        fx_copy(0, i).wait_send()
        fx_copy(1, i).wait_send()
        fq_copy(i).wait_send()
        for j in range(4):
            fs_copy(j, i).wait_send()
    for w in (0, 1):
        sb_copy(w).wait_send()
        pre_copies[w].wait_send()
        plain[w].wait_send()
        merge[w].wait_send()


def local(
    hidden_in, attn_gain, w_qkv, qkv_scale, q_gain, k_gain, key_cache, value_cache, lengths, w_out, out_scale,
    mlp_gain, w_gate, w_up, gate_scale, up_scale, w_down, down_scale,
):
    def quarters(w):
        return jnp.pad(w.reshape(40, 4, HID), ((0, 0), (0, 0), (0, PAD - HID)))

    gu4 = jnp.concatenate([quarters(w_gate), quarters(w_up)], axis=2).transpose(1, 0, 2)
    dn4 = jnp.pad(w_down.reshape(4, 50, 160), ((0, 0), (0, 6), (0, 0)))

    def padded(v):
        return jnp.pad(v.reshape(4, HID), ((0, 0), (0, PAD - HID)))

    gsc = jnp.concatenate([padded(gate_scale), padded(up_scale)], axis=1)
    freq = jnp.arange(64, dtype=F32)
    inverse = jnp.exp(freq * (-math.log(ROPE) / 64))
    angle = lengths[0].astype(F32)[:, None] * inverse[None, :]
    cos, sin = jnp.cos(angle), jnp.sin(angle)
    ctab = jnp.tile(jnp.concatenate([cos, cos], axis=1), (2, 1))
    stab = jnp.tile(jnp.concatenate([-sin, sin], axis=1), (2, 1))
    ltab = jnp.broadcast_to(jnp.tile(lengths[0], 2)[:, None], (8, HEAD))
    gains = jnp.stack([q_gain, k_gain])
    V, S = pltpu.VMEM, pltpu.SemaphoreType.DMA
    scratch = [
        V((ROWS, 384), F32), V((16, 4, 384), F32), V((16, 4, 384), F32), V((160, HEAD), F32), V((32, HEAD), F32),
        V((YS, 16, HEAD), BF), V((256, HEAD), BF), V((64, HALF), jnp.int32), V((512, HALF), BF), V((ROWS, HALF), BF),
        V((YS, 32, 640), BF), V((ALL, D), BF), V((4, ALL, 1280), BF), V((ZS, 160, 512), jnp.int32),
        V((4, 56, 160), jnp.int32), V((ZS, 56, 640), jnp.int32), V((4, 1280, 512), BF), V((256, D), BF),
        V((ALL, D), BF), V((2, ROWS, D), BF),
        V((2, ROWS, 1280), BF), V((2, ROWS, 1280), BF), V((2, ROWS, 1280), BF), V((2, ROWS, 1280), BF),
        V((2, ROWS, 1280), BF), V((2, ROWS, 1280), BF), V((ROWS, HALF), BF), V((YS, ROWS, 384), BF),
        S((2, 4)), S((2, 4)), S, S, S((2, 4, 2)), S((2, 4, 2)), S((16,)), S((16,)), S((16,)), S((16,)),
        S((8,)), S((8,)), S((8,)), S((8,)), S((2, 8)), S((2, 8)), S((8,)), S((8,)), S((4, 8)), S((4, 8)),
        S((2,)), S((2,)), S((2,)), S((2,)), S((2, 2)), S((2, 2)), S((8,)), S((8,)),
    ]
    return pl.pallas_call(
        kernel,
        out_shape=jax.ShapeDtypeStruct((ROWS, 320), BF),
        in_specs=[pl.BlockSpec(memory_space=pltpu.VMEM)] * 17,
        out_specs=pl.BlockSpec(memory_space=pltpu.VMEM),
        scratch_shapes=scratch,
        compiler_params=pltpu.CompilerParams(
            collective_id=0, has_side_effects=True, vmem_limit_bytes=60 * 1024 * 1024
        ),
        name="layer",
    )(
        hidden_in, attn_gain[None], w_qkv, qkv_scale[None], gains, key_cache[0], value_cache[0], ctab, stab, ltab,
        w_out, out_scale[None], mlp_gain[None], gu4, gsc, dn4, down_scale[None],
    )


def solution(mesh):
    return jax.shard_map(
        local,
        mesh=mesh,
        in_specs=(
            P(("grp", "src"), None),
            P(),
            P(None, "tp"),
            P("tp"),
            P(),
            P(),
            P(("grp", "src"), "tp", None, None),
            P(("grp", "src"), "tp", None, None),
            P(("grp", "src"), "tp"),
            P("tp", None),
            P(),
            P(),
            P(("grp", "src"), "tp"),
            P(("grp", "src"), "tp"),
            P("tp"),
            P("tp"),
            P("tp", ("grp", "src")),
            P(),
        ),
        out_specs=P(("grp", "src"), "tp"),
        check_vma=False,
    )
```

profile of v0, /device:TPU:6, one launch (start us, length us, event | category | flops | bytes accessed | tf_op | source)
XLA Modules:
  0.0 126.6 jit_solution(14663849282881756544)
XLA Ops:
  0.0 0.0 copy-start.1
  0.0 0.7 bitcast_convert_fusion
  0.7 1.4 %pad_maximum_fusion.2.gains = f32[2,128]{1,0:T(2,128)} fusion(f32[1,128]{1,0:T(1,128)} %bitcast.22, f32[1,128]{1,0:T(1,128)} %bitcast.23), kind=kLoop, calls=%fused_computation.9 | loop fusion | flops 256 | bytes 2048 | tf_op jit(solution)/shard_map/stack | solution.py:586
  2.1 0.7 tile.27
  2.8 0.1 broadcast_in_dim.26
  2.8 1.3 %broadcast_in_dim.25.qscale = f32[1,320]{1,0:T(1,128)} reshape(f32[320]{0:T(512)} %param.21) | data formatting | bytes 2560 | tf_op jit(solution)/shard_map/broadcast_in_dim | solution.py:611
  4.1 0.7 broadcast_in_dim.27.ltab
  4.8 0.8 reshape.36
  5.5 0.8 reshape.37
  6.3 0.6 select_maximum_fusion.gsc
  6.9 0.1 fusion.1
  7.0 0.1 pad_maximum_fusion
  7.1 0.6 tile.10
  7.7 0.6 tile.12
  8.3 1.1 reshape.34
  9.4 1.1 reshape.35
  10.5 0.8 fusion.gu4
  11.3 0.0 copy-done.1
  11.3 0.1 copy.23
  11.5 0.7 pad.22.dn4
  12.2 0.0 copy-done
  12.2 1.8 %copy.24.wq = s32[1280,320]{1,0:T(8,128)} copy(s32[1280,320]{0,1:T(8,128)S(1)} %copy-done) | data formatting | bytes 3276800 | tf_op args[2]
  14.0 111.1 %layer.1 = bf16[64,320]{1,0:T(8,128)(2,1)} custom-call(bf16[64,5120]{1,0:T(8,128)(2,1)} %hid.1, f32[1,5120]{1,0:T(1,128)} %bitcast.16, s32[1280,320]{1,0:T(8,128)} %copy.24.wq, f32[1,320]{1,0:T(1,128)} %broadcast_in_dim.25.qscale, f32[2,128]{1,0:T(2,128)} %pad_maximum_fusion.2.gains, bf16[4,128,512]{2,1,0:T(8,128)(2,1)} %bitcast.14, ...), custom_call_target="tpu_custom_call" | custom-call | tf_op jit(solution)/shard_map/layer/pallas_call | solution.py:600
  125.1 1.4 %copy.26 = bf16[64,320]{1,0:T(8,128)(2,1)} copy(bf16[64,320]{1,0:T(8,128)(2,1)} %layer.1) | data formatting | bytes 81920
  (5 shorter events, 0.1 us)
Async XLA Ops:
  0.0 11.3 %copy-start.1 = (s32[200,160]{0,1:T(8,128)S(1)}, s32[200,160]{0,1:T(8,128)}, u32[]{:S(2)}) copy-start(s32[200,160]{0,1:T(8,128)} %param.34) | copy-start | bytes 384004
  0.7 11.5 %copy-start = (s32[1280,320]{0,1:T(8,128)S(1)}, s32[1280,320]{0,1:T(8,128)}, u32[]{:S(2)}) copy-start(s32[1280,320]{0,1:T(8,128)} %param.20) | copy-start | bytes 4915204
where the time goes:
time: 128 us; the launch traced here: 127 us
  Pallas kernels  111 us (87%)
  local copies, waits for them, and re-layouts  11.7 us (9%)
  other arithmetic  3.68 us (3%)
    pallas_call x1, Pallas kernels, local(): pl.pallas_call(kernel, out_shape=jax.ShapeDtypeStruct((ROWS, 320), BF), i...  111 us
    unnamed x7, local copies, waits for them, and re-layouts  3.34 us

commit v1 on v0

v1 whole, which is shorter than its diff:
```python
import math

import jax
import jax.numpy as jnp
from jax import lax
from jax.experimental import pallas as pl
from jax.experimental.pallas import tpu as pltpu
from jax.sharding import PartitionSpec as P

D = 5120
HALF = 2560
HEADS = 32
KV = 4
HEAD = 128
ROWS = 64
ALL = 256
YS = 8
ZS = 8
HID = 200
PAD = 256
EPS = 1e-06
ROPE = 1000000.0
MESH = pl.DeviceIdType.MESH
F32 = jnp.float32
BF = jnp.bfloat16
NEAR = (0, 1, 7, 2, 6, 3, 5, 4)


def mo(value, k):
    return pl.multiple_of(value, k)


def byte_of(words, k):
    return jnp.right_shift(jnp.left_shift(words, 24 - 8 * k), 24).astype(F32).astype(BF)


def one_hot(n, used, stride):
    row = lax.broadcasted_iota(jnp.int32, (n, n), 0)
    col = lax.broadcasted_iota(jnp.int32, (n, n), 1)
    shift = stride.bit_length() - 1
    k, r = jnp.right_shift(col, shift), jnp.bitwise_and(col, stride - 1)
    return jnp.where((row == 4 * r + k) & (r < used), 1.0, 0.0).astype(BF)


def dot(a, b):
    return jnp.dot(a, b, preferred_element_type=F32)


def kernel(
    hid, again, wq_hbm, qscale, qgain, kgain, kc_hbm, vc_hbm, lens, wout, oscale, mgain, wgate, wup, gscale, uscale,
    wdown, dscale,
    out,
    wq, kc, vc, woh, p512, vec, gsc, stage, gu4, dn4, bsend, brecv, qs, vs, hsend, hrecv, wo_r, wo, pm, rs, X, xk, ssq,
    gub, dnp, dnb, dns, wg, wd, actr, pd, pre, smerge, rplain, rmerge, u, yr,
    ld, w1s, w1r, wos, wor, zs, zr, ns, nr, bs, br, hs, hr, rss, rsr, fys, fyr, fxs, fxr, fqs, fqr, fss, fsr,
    acs, acr, xps, xpr, xas, xar, xms, xmr, yss, ysr,
):
    z = lax.axis_index("grp")
    tp = lax.axis_index("tp")
    src = lax.axis_index("src")
    xl, y = tp // YS, tp % YS
    xh, core = src // 2, src % 2
    x = xh * 2 + xl

    def at_x(xx, cc):
        return {"tp": (xx % 2) * YS + y, "src": (xx // 2) * 2 + cc}

    xp, xm, xo = (x + 1) % 4, (x + 3) % 4, (x + 2) % 4
    PLUS, MINUS = at_x(xp, core), at_x(xm, core)
    SIB = {"src": xh * 2 + 1 - core}
    ZP, ZM = {"grp": (z + 1) % ZS}, {"grp": (z + ZS - 1) % ZS}

    def rcopy(a, b, s, r, to):
        return pltpu.make_async_remote_copy(
            src_ref=a, dst_ref=b, send_sem=s, recv_sem=r, device_id=to, device_id_type=MESH
        )

    load_wq = [
        pltpu.make_async_copy(wq_hbm.at[pl.ds(i * 640, 640), :], wq.at[pl.ds(i * 640, 640), :], ld.at[i]) for i in (0, 1)
    ]
    load_kc = pltpu.make_async_copy(kc_hbm.at[0], kc, ld.at[2])
    load_vc = pltpu.make_async_copy(vc_hbm.at[0], vc, ld.at[3])
    load_wo = pltpu.make_async_copy(wout.at[:, pl.ds(mo(xl * HALF, 128), HALF)], woh, ld.at[4])
    for c in load_wq:
        c.start()
    load_kc.start()
    load_vc.start()
    load_wo.start()

    barrier = pltpu.get_barrier_semaphore()

    def greet_tp(d, _):
        pl.semaphore_signal(barrier, inc=1, device_id={"tp": (tp + d) % 16}, device_id_type=MESH)
        return 0

    def greet_src(d, _):
        pl.semaphore_signal(barrier, inc=1, device_id={"src": (src + d) % 4}, device_id_type=MESH)
        return 0

    lax.fori_loop(1, 16, greet_tp, 0)
    lax.fori_loop(1, 4, greet_src, 0)
    across = {"tp": (1 - xl) * YS + y, "src": (1 - xh) * 2 + core}
    for to in (across, ZP, ZM):
        pl.semaphore_signal(barrier, inc=1, device_id=to, device_id_type=MESH)

    for s in range(4):
        piece = jnp.concatenate([wgate[:, HID * s : HID * s + HID], wup[:, HID * s : HID * s + HID]], axis=1)
        gu4[s] = piece[:, :384]
        dn4[s] = jnp.zeros((56, 256), jnp.int32)
        dn4[s, 0:50, 0:160] = wdown[50 * s : 50 * s + 50, :]
        dn4[s, 0:40, 160:176] = piece[:, 384:400]
    gub[0, pl.ds(mo(src * 40, 8), 40), :] = gu4[src]
    dnp[src] = dn4[src]
    p512[...] = one_hot(512, 128, 128)
    vec[0:1, :] = again[...][None, :]
    vec[1:2, :] = mgain[...][None, :]
    vec[2:3, :] = oscale[...][None, :]
    vec[3:4, :] = dscale[...][None, :]

    total = jnp.zeros((ROWS, 1), F32)
    for g in range(10):
        v = hid[:, g * 512 : (g + 1) * 512].astype(F32)
        total = total + jnp.sum(v * v, axis=1, keepdims=True)
    rms = lax.rsqrt(total * (1.0 / D) + EPS)
    stage[...] = jnp.broadcast_to(rms, (ROWS, 384))

    def qkv_group(g, acc):
        at = pl.ds(mo(g * 512, 512), 512)
        v = (hid[:, at].astype(F32) * stage[:, 0:1] * vec[0:1, at]).astype(BF)
        v = dot(v, p512[...]).astype(BF)
        w = wq[pl.ds(mo(g * 128, 128), 128), :]
        for k in range(4):
            acc = acc + dot(v[:, k * 128 : (k + 1) * 128], byte_of(w, k))
        return acc

    load_wq[0].wait()
    acc = lax.fori_loop(0, 5, qkv_group, jnp.zeros((ROWS, 320), F32))
    pl.semaphore_wait(barrier, 21)

    def w1_gu(d):
        s2 = (src + d) % 4
        return rcopy(
            gu4.at[s2], gub.at[0, pl.ds(mo(src * 40, 8), 40), :], w1s.at[0, d], w1r.at[0, src], {"src": s2}
        )

    def w1_dn(d):
        s2 = (src + d) % 4
        return rcopy(dn4.at[s2], dnp.at[src], w1s.at[1, d], w1r.at[1, src], {"src": s2})

    for d in (1, 2, 3):
        w1_gu(d).start()
        w1_dn(d).start()

    load_wq[1].wait()
    acc = lax.fori_loop(5, 10, qkv_group, acc)
    qkv = (acc * qscale[...][None, :]).astype(BF).astype(F32)
    stage[...] = jnp.zeros((ROWS, 384), F32)
    stage[:, :320] = qkv
    odd_y = (y % 2) == 1
    placed = stage[...]
    placed = jnp.where(odd_y, pltpu.roll(placed, 64, 1), placed)
    for t in range(16):
        bsend[t] = placed[4 * t : 4 * t + 4, :]

    def b_copy(d):
        to = (tp + d) % 16
        return rcopy(bsend.at[to], brecv.at[tp], bs.at[to], br.at[tp], {"tp": to})

    def start_b(d, _):
        b_copy(d).start()
        return 0

    def wait_b(d, _):
        frm = (tp + d) % 16
        rcopy(bsend.at[frm], brecv.at[frm], bs.at[frm], br.at[frm], {"tp": frm}).wait_recv()
        return 0

    lax.fori_loop(1, 16, start_b, 0)
    wo_side = (x + 1 + 2 * core) % 4
    wo_copy = rcopy(
        wout.at[:, pl.ds(mo((1 - xl) * HALF, 128), HALF)], wo_r, wos, wor, at_x(wo_side, core)
    )
    wo_copy.start()
    brecv[pl.ds(tp, 1)] = bsend[pl.ds(tp, 1)]

    def w1_in(d):
        s2 = (src + d) % 4
        rcopy(gu4.at[s2], gub.at[0, pl.ds(mo(s2 * 40, 8), 40), :], w1s.at[0, d], w1r.at[0, s2], {"src": s2}).wait_recv()
        rcopy(dn4.at[s2], dnp.at[s2], w1s.at[1, d], w1r.at[1, s2], {"src": s2}).wait_recv()

    def assemble(h):
        one, two = dnp[2 * h], dnp[2 * h + 1]
        dnb[0, h] = jnp.concatenate(
            [one[:, :160], two[:, :160], one[:, 160:192], two[:, 160:192]], axis=1
        )

    def ring(h, step, way):
        a = step - 1 if way == 0 else (9 - step) % 8
        b = step if way == 0 else 8 - step
        to = ZP if way == 0 else ZM
        if step == 4:
            n, off, d_at = (40, 0, slice(0, 32)) if way == 0 else (40, 40, slice(32, 56))
        else:
            n, off, d_at = 80, 0, slice(0, 56)
        at = pl.ds(mo(h * 80 + off, 8), n)
        one = rcopy(gub.at[a, at, :], gub.at[b, at, :], zs.at[h, way, step - 1, 0], zr.at[h, way, step - 1, 0], to)
        two = rcopy(
            dnb.at[a, h, d_at, :], dnb.at[b, h, d_at, :], zs.at[h, way, step - 1, 1], zr.at[h, way, step - 1, 1], to
        )
        return one, two

    def ring_start(h, step):
        for way in (0, 1):
            for c in ring(h, step, way):
                c.start()

    def ring_wait(h, step):
        for way in (0, 1):
            for c in ring(h, step, way):
                c.wait_recv()

    def to_sib(slot):
        return rcopy(dnb.at[slot], dns.at[slot], ns.at[slot], nr.at[slot], SIB)

    def hop(step):
        for h in (xh, 1 - xh):
            ring_wait(h, step)
            if step < 4:
                ring_start(h, step + 1)
        if step < 4:
            to_sib(step).start()
            to_sib(8 - step).start()
        else:
            to_sib(4).start()

    def unpack_down(ref, slot, which):
        zz = (z + ZS - slot) % ZS
        w = jnp.concatenate([ref[slot, 0, :, :320], ref[slot, 1, :, :320]], axis=1)
        for k in range(4):
            wd[which, k * 64 : k * 64 + 56, pl.ds(mo(zz * 640, 128), 640)] = byte_of(w, k)

    lane40 = lax.broadcasted_iota(jnp.int32, (40, 128), 1)

    def unpack(slot):
        zz = (z + ZS - slot) % ZS

        def rows(i, _):
            w = gub[slot, pl.ds(mo(i * 32, 32), 32), :]
            for k in range(4):
                wg[k, pl.ds(mo(zz * 160 + i * 32, 32), 32), 0:384] = byte_of(w, k)
            return 0

        lax.fori_loop(0, 5, rows, 0)
        tails = []
        for s in range(4):
            t = dnb[slot, s // 2, 0:40, 256:384]
            t = pltpu.roll(t, 64 - 32 * (s % 2), 1)
            tails.append(jnp.where(lane40 < 16, t, 0))
        tails = jnp.concatenate(tails, axis=0)
        for k in range(4):
            wg[k, pl.ds(mo(zz * 160, 32), 160), 384:512] = byte_of(tails, k)
        unpack_down(dnb, slot, 0)

    def unpack_sib(slot):
        to_sib(slot).wait_recv()
        unpack_down(dns, slot, 1)

    rcopy(
        gu4.at[0], gub.at[0, pl.ds(mo((src + 1 - 2 * core) * 40, 8), 40), :], w1s.at[0, 1],
        w1r.at[0, src + 1 - 2 * core], SIB,
    ).wait_recv()
    rcopy(dn4.at[0], dnp.at[src + 1 - 2 * core], w1s.at[1, 1], w1r.at[1, src + 1 - 2 * core], SIB).wait_recv()
    assemble(xh)
    ring_start(xh, 1)
    wd[...] = jnp.zeros(wd.shape, BF)

    def unpack_wo(ref, base):
        def cols(i, _):
            at = pl.ds(mo(i * 640, 128), 640)
            for hl in range(2):
                w = ref[hl * 32 : hl * 32 + 32, at]
                for k in range(4):
                    wo[pl.ds(mo(base + hl * 128 + k * 32, 32), 32), at] = byte_of(w, k)
            return 0

        lax.fori_loop(0, 4, cols, 0)

    load_wo.wait()
    unpack_wo(woh, xl * 256)
    far = (1 - xh) * 2
    for s2 in (far, far + 1):
        rcopy(gu4.at[0], gub.at[0, pl.ds(mo(s2 * 40, 8), 40), :], w1s.at[0, 2], w1r.at[0, s2], {"src": s2}).wait_recv()
        rcopy(dn4.at[0], dnp.at[s2], w1s.at[1, 2], w1r.at[1, s2], {"src": s2}).wait_recv()
    assemble(1 - xh)
    ring_start(1 - xh, 1)
    to_sib(0).start()
    unpack(0)
    load_kc.wait()
    load_vc.wait()
    half = lax.broadcasted_iota(jnp.int32, (8, HEAD), 1)
    pair = jnp.bitwise_and(lax.broadcasted_iota(jnp.int32, (8, HEAD), 0), 3)
    length = jnp.full((8, HEAD), lens[0, 0], jnp.int32)
    for b in range(1, 4):
        length = jnp.where(pair == b, lens[0, b], length)
    freq = jnp.exp(jnp.bitwise_and(half, 63).astype(F32) * (-math.log(ROPE) / 64))
    angle = length.astype(F32) * freq
    ctab = jnp.cos(angle)
    stab = jnp.sin(angle)
    stab = jnp.where(half < 64, -stab, stab)

    lax.fori_loop(1, 16, wait_b, 0)
    lane = lax.broadcasted_iota(jnp.int32, (4, HEAD), 1)
    for p in range(8):
        even, odd = brecv[2 * p], brecv[2 * p + 1]
        pieces = (
            even[:, 0:128],
            even[:, 128:256],
            jnp.where(lane < 64, even[:, 256:384], odd[:, 0:128]),
            odd[:, 128:256],
            odd[:, 256:384],
        )
        for j, piece in enumerate(pieces):
            h = 5 * p + j
            if h < HEADS:
                qs[4 * h : 4 * h + 4, :] = piece
            elif h < HEADS + KV:
                at = 128 + 8 * (h - HEADS)
                qs[at : at + 4, :] = piece
                qs[at + 4 : at + 8, :] = piece
            else:
                at = 8 * (h - HEADS - KV)
                vs[at : at + 4, :] = piece
                vs[at + 4 : at + 8, :] = piece
    v = qs[...]
    v = v * lax.rsqrt(jnp.mean(v * v, axis=1, keepdims=True) + EPS)
    row = lax.broadcasted_iota(jnp.int32, (160, HEAD), 0)
    v = v * jnp.where(row < 128, qgain[...][None, :], kgain[...][None, :])
    turned = pltpu.roll(v, 64, 1)
    v = v.reshape(20, 8, HEAD) * ctab[None] + turned.reshape(20, 8, HEAD) * stab[None]
    v = v.reshape(160, HEAD).astype(BF)
    scale = 1.0 / math.sqrt(HEAD)
    seq = jnp.bitwise_and(lax.broadcasted_iota(jnp.int32, (32, HEAD), 0), 3)
    live = jnp.where(half < length, 1.0, 0.0)
    live = jnp.broadcast_to(live[None], (4, 8, HEAD)).reshape(32, HEAD) > 0.5
    heads = []
    for g in range(KV):
        q = v[32 * g : 32 * g + 32]
        newk = v[128 + 8 * g : 136 + 8 * g].astype(F32)
        own = jnp.sum((q.astype(F32).reshape(4, 8, HEAD) * newk[None]).reshape(32, HEAD), axis=1, keepdims=True)
        own = own * scale
        s = jnp.zeros((32, HEAD), F32)
        for b in range(4):
            sb = lax.dot_general(
                q, kc[b, :, g * 128 : (g + 1) * 128], (((1,), (1,)), ((), ())), preferred_element_type=F32
            )
            s = jnp.where(seq == b, sb, s)
        s = jnp.where(live, s * scale, -jnp.inf)
        top = jnp.maximum(jnp.max(s, axis=1, keepdims=True), own)
        e = jnp.exp(s - top)
        own_e = jnp.exp(own - top)
        den = jnp.sum(e, axis=1, keepdims=True) + own_e
        newv = vs[8 * g : 8 * g + 8, :]
        low = own_e.astype(BF).astype(F32)
        num = (low.reshape(4, 8, 1) * newv[None]).reshape(32, HEAD)
        for b in range(4):
            eb = jnp.where(seq == b, e, 0.0).astype(BF)
            num = num + dot(eb, vc[b, :, g * 128 : (g + 1) * 128])
        heads.append(num / den)
    for yy in range(YS):
        g, at = yy // 4, 8 * (yy % 4)
        hsend[yy] = jnp.concatenate([heads[g][at : at + 8], heads[g + 2][at : at + 8]], axis=0).astype(BF)

    def h_slot(t):
        return hrecv.at[pl.ds(mo(t * 16, 16), 16), :]

    def h_copy(d):
        to = (tp + d) % 16
        return rcopy(hsend.at[to % YS], h_slot(tp), hs.at[to], hr.at[tp], {"tp": to})

    def start_h(d, _):
        h_copy(d).start()
        return 0

    def wait_h(d, _):
        frm = (tp + d) % 16
        rcopy(hsend.at[frm % YS], h_slot(frm), hs.at[frm], hr.at[frm], {"tp": frm}).wait_recv()
        return 0

    lax.fori_loop(1, 16, start_h, 0)
    hrecv[pl.ds(mo(tp * 16, 16), 16), :] = hsend[y]

    wo_copy.wait_recv()
    unpack_wo(wo_r, (1 - xl) * 256)
    hop(1)

    lax.fori_loop(1, 16, wait_h, 0)
    P128 = one_hot(128, 32, 32)
    got = hrecv[...]
    t = lax.broadcasted_iota(jnp.int32, (ROWS, 256), 0)
    c = lax.broadcasted_iota(jnp.int32, (ROWS, 256), 1)
    zcat = []
    for hl in range(4):
        want = jnp.right_shift(t, 2) * 16 + hl * 4 + jnp.bitwise_and(t, 3)
        pick = jnp.where(c == want, 1.0, 0.0).astype(BF)
        zcat.append(dot(dot(pick, got).astype(BF), P128).astype(BF))
    zcat = jnp.concatenate(zcat, axis=1)

    def part(yy):
        return pl.ds(mo(32 * (yy // 4), 32), 32), pl.ds(mo(640 * (yy % 4), 128), 640)

    for cb in range(4):
        pm[:, cb * 640 : cb * 640 + 640] = dot(zcat, wo[:, cb * 640 : cb * 640 + 640]).astype(BF)

    def r_copy(d):
        to = (y + d) % YS
        a, b = part(to)
        return rcopy(pm.at[a, b], rs.at[y], rss.at[to], rsr.at[y], {"tp": xl * YS + to})

    def wait_r(d, _):
        frm = (y + d) % YS
        a, b = part(frm)
        rcopy(pm.at[a, b], rs.at[frm], rss.at[frm], rsr.at[frm], {"tp": xl * YS + frm}).wait_recv()
        return 0

    for d in NEAR[:0:-1]:
        r_copy(d).start()
    a, b = part(y)
    rs[y] = pm[a, b]
    unpack(1)
    unpack(7)
    unpack_sib(0)
    hop(2)

    lax.fori_loop(1, YS, wait_r, 0)
    mid = rs[0].astype(F32)
    for i in range(1, YS):
        mid = mid + rs[i].astype(F32)
    cols = pl.ds(mo(xl * HALF + 640 * (y % 4), 128), 640)
    mid = hid[a, cols].astype(F32) + mid * vec[2:3, cols]
    X[pl.ds(mo(src * 64 + 32 * (y // 4), 32), 32), cols] = mid.astype(BF)

    def blk(xx, cc, yy):
        r0 = ((xx // 2) * 2 + cc) * 64 + 32 * (yy // 4)
        c0 = (xx % 2) * HALF + 640 * (yy % 4)
        return X.at[pl.ds(mo(r0, 32), 32), pl.ds(mo(c0, 128), 640)]

    def fy_copy(d):
        to = (y + d) % YS
        return rcopy(blk(x, core, y), blk(x, core, y), fys.at[to], fyr.at[y], {"tp": xl * YS + to})

    for d in NEAR[1:]:
        fy_copy(d).start()

    def fx_copy(way, i):
        b0 = blk(x, core, (y + i) % YS)
        return rcopy(b0, b0, fxs.at[way, i], fxr.at[way, i], PLUS if way == 0 else MINUS)

    def fx_in(way, i):
        b0 = blk(xm if way == 0 else xp, core, (y + i) % YS)
        return rcopy(b0, b0, fxs.at[way, i], fxr.at[way, i], MINUS if way == 0 else PLUS)

    def fq_copy(i):
        way = i % 2
        b0 = blk(xm if way == 0 else xp, core, (y + i) % YS)
        return rcopy(b0, b0, fqs.at[i], fqr.at[i], PLUS if way == 0 else MINUS)

    def fq_in(i):
        b0 = blk(xo, core, (y + i) % YS)
        return rcopy(b0, b0, fqs.at[i], fqr.at[i], MINUS if i % 2 == 0 else PLUS)

    froms = (x, xm, xp, xo)

    def fs_copy(j, i):
        b0 = blk(froms[j], core, (y + i) % YS)
        return rcopy(b0, b0, fss.at[j, i], fsr.at[j, i], SIB)

    def fs_in(j, i):
        b0 = blk(froms[j], 1 - core, (y + i) % YS)
        return rcopy(b0, b0, fss.at[j, i], fsr.at[j, i], SIB)

    def gained(xx, cc):
        at = pl.ds(mo(((xx // 2) * 2 + cc) * 64, 64), 64)
        total = jnp.zeros((64, 1), F32)
        for g in range(5):
            c0 = (xx % 2) * HALF + g * 512
            cs = pl.ds(mo(c0, 128), 512)
            v = X[at, cs].astype(F32)
            total = total + jnp.sum(v * v, axis=1, keepdims=True)
            v = dot((v * vec[1:2, cs]).astype(BF), p512[...]).astype(BF)
            to = pl.ds(mo((xx % 2) * 640 + g * 128, 128), 128)
            for k in range(4):
                xk[k, at, to] = v[:, k * 128 : (k + 1) * 128]
        ssq[xx % 2, at, :] = jnp.broadcast_to(total, (64, HEAD))

    for n, i in enumerate(NEAR):
        yy = (y + i) % YS
        if i:
            b0 = blk(x, core, yy)
            rcopy(b0, b0, fys.at[yy], fyr.at[yy], {"tp": xl * YS + yy}).wait_recv()
        fx_copy(0, i).start()
        fx_copy(1, i).start()
        fs_copy(0, i).start()
        if n == 3:
            unpack(2)
            unpack(6)
            unpack_sib(1)
            unpack_sib(7)
            hop(3)
    gained(x, core)
    for i in NEAR:
        fx_in(0, i).wait_recv()
        fx_in(1, i).wait_recv()
        fq_copy(i).start()
        fs_copy(1, i).start()
        fs_copy(2, i).start()
    gained(xm, core)
    gained(xp, core)
    unpack(3)
    unpack(5)
    unpack_sib(2)
    unpack_sib(6)
    for i in NEAR:
        fs_in(0, i).wait_recv()
    gained(x, 1 - core)
    hop(4)
    unpack(4)
    unpack_sib(3)
    unpack_sib(5)
    for i in NEAR:
        fq_in(i).wait_recv()
        fs_copy(3, i).start()
    gained(xo, core)
    for j in (1, 2, 3):
        for i in NEAR:
            fs_in(j, i).wait_recv()
        gained(froms[j], 1 - core)
    gsc[...] = jnp.zeros((8, 1024), F32)
    gsc[0:1, :800] = gscale[...][None, :]
    gsc[1:2, :800] = uscale[...][None, :]
    shifted = gsc[...]
    mine = shifted
    for s in range(1, 4):
        mine = jnp.where(src == s, pltpu.roll(shifted, 1024 - HID * s, 1), mine)
    both = dot(xk[0], wg[0])
    for k in range(1, 4):
        both = both + dot(xk[k], wg[k])
    rms = lax.rsqrt((ssq[0, :, 0:1] + ssq[1, :, 0:1]) * (1.0 / D) + EPS)
    gate = both[:, :PAD] * rms * mine[0:1, :PAD]
    up = pltpu.roll(both, 512 - HID, 1)[:, :PAD] * rms * mine[1:2, :PAD]
    used = lax.broadcasted_iota(jnp.int32, (1, PAD), 1) < HID
    act = jnp.where(used, gate / (1.0 + jnp.exp(-gate)) * up, 0.0).astype(BF)
    act = dot(act, one_hot(PAD, HID // 4, 64)).astype(BF)
    xk[0, :, :PAD] = act

    def act_rows(h, cc):
        return pl.ds(mo((h * 2 + cc) * 64, 64), 64)

    def ac_copy(h):
        return rcopy(xk.at[0, act_rows(h, 1 - core), 0:PAD], actr.at[h], acs.at[h], acr.at[h], SIB)

    for h in (0, 1):
        ac_copy(h).start()
    unpack_sib(4)
    for h in (0, 1):
        ac_copy(h).wait_recv()
    lhs = [
        jnp.concatenate([xk[0, act_rows(0, core), 0:PAD], xk[0, act_rows(1, core), 0:PAD]], axis=0),
        jnp.concatenate([actr[0], actr[1]], axis=0),
    ]

    def down(c0):
        def some(n, _):
            at = pl.ds(mo(c0 + n * 640, 128), 640)
            r = dot(lhs[0], wd[0, :, at]) + dot(lhs[1], wd[1, :, at])
            pd[:, at] = r.astype(BF)
            return 0

        lax.fori_loop(0, 2, some, 0)

    sides = (PLUS, MINUS)
    nexts = (xp, xm)

    def slab(xx, q, w):
        rows = pl.ds(mo((xx // 2) * 64, 64), 64)
        return rows, pl.ds(mo((xx % 2) * HALF + q * 1280 + w * 640, 128), 640)

    def pre_copy(q, w):
        a, b = slab(xo, q, w)
        return rcopy(pd.at[a, b], pre.at[q, w], xps.at[q, w], xpr.at[q, w], sides[w])

    def plain_copy(q, w):
        a, b = slab(nexts[w], q, 1 - w)
        return rcopy(pd.at[a, b], rplain.at[q, w], xas.at[q, w], xar.at[q, w], sides[w])

    def merge_copy(q, w):
        return rcopy(smerge.at[q, w], rmerge.at[q, w], xms.at[q, w], xmr.at[q, w], sides[w])

    def merge(q):
        for w in (0, 1):
            pre_copy(q, w).wait_recv()
            a, b = slab(nexts[w], q, w)
            smerge[q, w] = (pd[a, b].astype(F32) + pre[q, w].astype(F32)).astype(BF)
            merge_copy(q, w).start()

    def window(yy):
        return pl.ds(mo(320 * yy - 64 * (yy % 2), 128), 384)

    def finish(q):
        for w in (0, 1):
            plain_copy(q, w).wait_recv()
        for w in (0, 1):
            merge_copy(q, w).wait_recv()
            a, b = slab(x, q, w)
            v = pd[a, b].astype(F32) + rplain[q, 1 - w].astype(F32) + rmerge[q, w].astype(F32)
            u[:, q * 1280 + w * 640 : q * 1280 + w * 640 + 640] = v.astype(BF)

    def y_copy(to):
        return rcopy(u.at[:, window(to)], yr.at[y], yss.at[to], ysr.at[y], {"tp": xl * YS + to})

    def y_sends(q):
        for i in range(4):
            to = 4 * q + i

            @pl.when(to != y)
            def _():
                y_copy(to).start()

            @pl.when(to == y)
            def _():
                yr[y] = u[:, window(to)]

    down(xl * HALF)
    for w in (0, 1):
        pre_copy(0, w).start()
    down((1 - xl) * HALF)
    for w in (0, 1):
        plain_copy(0, w).start()
    down(xl * HALF + 1280)
    for w in (0, 1):
        pre_copy(1, w).start()
    down((1 - xl) * HALF + 1280)
    for w in (0, 1):
        plain_copy(1, w).start()
    merge(0)
    merge(1)
    finish(0)
    y_sends(0)
    finish(1)
    y_sends(1)
    for d in NEAR[1:]:
        frm = (y + d) % YS
        rcopy(u.at[:, window(frm)], yr.at[frm], yss.at[frm], ysr.at[frm], {"tp": xl * YS + frm}).wait_recv()
    last = yr[0].astype(F32)
    for i in range(1, YS):
        last = last + yr[i].astype(F32)
    at = pl.ds(mo(xl * HALF + 320 * y - 64 * (y % 2), 128), 384)
    last = X[pl.ds(mo(src * 64, 64), 64), at].astype(F32) + last * vec[3:4, at]
    last = jnp.where(odd_y, pltpu.roll(last, 320, 1), last)
    out[...] = last[:, :320].astype(BF)

    for d in (1, 2, 3):
        w1_gu(d).wait_send()
        w1_dn(d).wait_send()
    wo_copy.wait_send()
    for h in (0, 1):
        for step in (1, 2, 3, 4):
            for way in (0, 1):
                for c in ring(h, step, way):
                    c.wait_send()
    for slot in range(ZS):
        to_sib(slot).wait_send()

    def sent_tp(d, _):
        b_copy(d).wait_send()
        h_copy(d).wait_send()
        return 0

    def sent_y(d, _):
        r_copy(d).wait_send()
        fy_copy(d).wait_send()
        y_copy((y + d) % YS).wait_send()
        return 0

    lax.fori_loop(1, 16, sent_tp, 0)
    lax.fori_loop(1, YS, sent_y, 0)
    for i in range(YS):
        fx_copy(0, i).wait_send()
        fx_copy(1, i).wait_send()
        fq_copy(i).wait_send()
        for j in range(4):
            fs_copy(j, i).wait_send()
    for w in (0, 1):
        ac_copy(w).wait_send()
        for q in (0, 1):
            pre_copy(q, w).wait_send()
            plain_copy(q, w).wait_send()
            merge_copy(q, w).wait_send()


def local(
    hidden_in, attn_gain, w_qkv, qkv_scale, q_gain, k_gain, key_cache, value_cache, lengths, w_out, out_scale,
    mlp_gain, w_gate, w_up, gate_scale, up_scale, w_down, down_scale,
):
    V, S = pltpu.VMEM, pltpu.SemaphoreType.DMA
    I32 = jnp.int32
    scratch = [
        V((1280, 320), I32), V((4, 128, 512), BF), V((4, 128, 512), BF), V((64, HALF), I32), V((512, 512), BF),
        V((8, D), F32), V((8, 1024), F32),
        V((ROWS, 384), F32), V((4, 40, 384), I32), V((4, 56, 256), I32),
        V((16, 4, 384), F32), V((16, 4, 384), F32), V((160, HEAD), F32), V((32, HEAD), F32),
        V((YS, 16, HEAD), BF), V((256, HEAD), BF), V((64, HALF), I32), V((512, HALF), BF), V((ROWS, HALF), BF),
        V((YS, 32, 640), BF), V((ALL, D), BF), V((4, ALL, 1280), BF), V((2, ALL, HEAD), F32),
        V((ZS, 160, 384), I32), V((4, 56, 256), I32), V((ZS, 2, 56, 384), I32), V((ZS, 2, 56, 384), I32),
        V((4, 1280, 512), BF), V((2, 256, D), BF), V((2, ROWS, PAD), BF), V((2 * ROWS, D), BF),
        V((2, 2, ROWS, 640), BF), V((2, 2, ROWS, 640), BF), V((2, 2, ROWS, 640), BF), V((2, 2, ROWS, 640), BF),
        V((ROWS, HALF), BF), V((YS, ROWS, 384), BF),
        S((5,)), S((2, 4)), S((2, 4)), S, S, S((2, 2, 4, 2)), S((2, 2, 4, 2)), S((8,)), S((8,)),
        S((16,)), S((16,)), S((16,)), S((16,)),
        S((8,)), S((8,)), S((8,)), S((8,)), S((2, 8)), S((2, 8)), S((8,)), S((8,)), S((4, 8)), S((4, 8)),
        S((2,)), S((2,)), S((2, 2)), S((2, 2)), S((2, 2)), S((2, 2)), S((2, 2)), S((2, 2)), S((8,)), S((8,)),
    ]
    vmem = pl.BlockSpec(memory_space=pltpu.VMEM)
    far = pl.BlockSpec(memory_space=pl.ANY)
    specs = [vmem] * 18
    for i in (2, 6, 7, 9):
        specs[i] = far
    specs[8] = pl.BlockSpec(memory_space=pltpu.SMEM)
    return pl.pallas_call(
        kernel,
        out_shape=jax.ShapeDtypeStruct((ROWS, 320), BF),
        in_specs=specs,
        out_specs=vmem,
        scratch_shapes=scratch,
        compiler_params=pltpu.CompilerParams(
            collective_id=0, has_side_effects=True, vmem_limit_bytes=60 * 1024 * 1024
        ),
        name="layer",
    )(
        hidden_in, attn_gain, w_qkv, qkv_scale, q_gain, k_gain, key_cache, value_cache, lengths, w_out, out_scale,
        mlp_gain, w_gate, w_up, gate_scale, up_scale, w_down, down_scale,
    )


def solution(mesh):
    return jax.shard_map(
        local,
        mesh=mesh,
        in_specs=(
            P(("grp", "src"), None),
            P(),
            P(None, "tp"),
            P("tp"),
            P(),
            P(),
            P(("grp", "src"), "tp", None, None),
            P(("grp", "src"), "tp", None, None),
            P(("grp", "src"), "tp"),
            P("tp", None),
            P(),
            P(),
            P(("grp", "src"), "tp"),
            P(("grp", "src"), "tp"),
            P("tp"),
            P("tp"),
            P("tp", ("grp", "src")),
            P(),
        ),
        out_specs=P(("grp", "src"), "tp"),
        check_vma=False,
    )
```

time: 128 us -> 101 us (0.79)
  the two profiles are of different devices: /device:TPU:6 before, /device:TPU:56 now
where the time goes in v1:
time: 101 us
  Pallas kernels  95.1 us (94%)
  local copies, waits for them, and re-layouts  5.95 us (6%)
    pallas_call x1, Pallas kernels, local(): pl.pallas_call(kernel, out_shape=jax.ShapeDtypeStruct((ROWS, 320), BF), i...  95.1 us
    unnamed x3, local copies, waits for them, and re-layouts  5.95 us

profile of v1, /device:TPU:56, one launch (start us, length us, event | category | flops | bytes accessed | tf_op | source)
XLA Modules:
  0.0 101.1 jit_solution(9715500657013315842)
XLA Ops:
  0.0 1.7 %copy.20.wdown = s32[200,160]{1,0:T(8,128)} copy(s32[200,160]{0,1:T(8,128)} %param.34) | data formatting | bytes 256000 | tf_op args[16]
  1.7 2.8 %copy.19.wq_hbm = s32[1280,320]{1,0:T(8,128)} copy(s32[1280,320]{0,1:T(8,128)} %param.20) | data formatting | bytes 3276800 | tf_op args[2]
  4.5 95.1 %layer.1 = bf16[64,320]{1,0:T(8,128)(2,1)} custom-call(bf16[64,5120]{1,0:T(8,128)(2,1)} %hid.1, f32[5120]{0:T(1024)} %again.1, s32[1280,320]{1,0:T(8,128)} %copy.19.wq_hbm, f32[320]{0:T(512)} %qscale.1, f32[128]{0:T(128)} %qgain.1, f32[128]{0:T(128)} %kgain.1, bf16[1,4,128,512]{3,2,1,0:T(8,128)(2,1)} %kc_hbm.1, bf16[1,4,128,512]{3,2,1,0:T(8,128)(2,1)} %vc_hbm.1, ...), custom_call_target="tpu_custom_call" | custom-call | tf_op jit(solution)/shard_map/layer/pallas_call | solution.py:728
  99.6 1.4 %copy.22 = bf16[64,320]{1,0:T(8,128)(2,1)} copy(bf16[64,320]{1,0:T(8,128)(2,1)} %layer.1) | data formatting | bytes 81920

commit v2 on v1

--- a/solution.py
+++ b/solution.py
@@ -47,9 +47,10 @@
 
 
 def kernel(
-    hid, again, wq_hbm, qscale, qgain, kgain, kc_hbm, vc_hbm, lens, wout, oscale, mgain, wgate, wup, gscale, uscale,
-    wdown, dscale,
+    hid_hbm, again_hbm, wq_hbm, qscale_hbm, qgain_hbm, kgain_hbm, kc_hbm, vc_hbm, lens, wout, oscale_hbm, mgain_hbm,
+    wgate_hbm, wup_hbm, gscale_hbm, uscale_hbm, wdown_hbm, dscale_hbm,
     out,
+    hid, again, qscale, qgain, kgain, oscale, mgain, wgate, wup, gscale, uscale, wdown, dscale,
     wq, kc, vc, woh, p512, vec, gsc, stage, gu4, dn4, bsend, brecv, qs, vs, hsend, hrecv, wo_r, wo, pm, rs, X, xk, ssq,
     gub, dnp, dnb, dns, wg, wd, actr, pd, pre, smerge, rplain, rmerge, u, yr,
     ld, w1s, w1r, wos, wor, zs, zr, ns, nr, bs, br, hs, hr, rss, rsr, fys, fyr, fxs, fxr, fqs, fqr, fss, fsr,
@@ -76,12 +77,18 @@
         )
 
     load_wq = [
-        pltpu.make_async_copy(wq_hbm.at[pl.ds(i * 640, 640), :], wq.at[pl.ds(i * 640, 640), :], ld.at[i]) for i in (0, 1)
+        pltpu.make_async_copy(wq_hbm.at[:, pl.ds(i * 640, 640)], wq.at[:, pl.ds(i * 640, 640)], ld.at[i]) for i in (0, 1)
     ]
     load_kc = pltpu.make_async_copy(kc_hbm.at[0], kc, ld.at[2])
     load_vc = pltpu.make_async_copy(vc_hbm.at[0], vc, ld.at[3])
     load_wo = pltpu.make_async_copy(wout.at[:, pl.ds(mo(xl * HALF, 128), HALF)], woh, ld.at[4])
-    for c in load_wq:
+    pairs = (
+        (hid_hbm, hid), (again_hbm, again), (wgate_hbm, wgate), (wup_hbm, wup), (wdown_hbm, wdown), (mgain_hbm, mgain),
+        (oscale_hbm, oscale), (dscale_hbm, dscale), (qscale_hbm, qscale), (qgain_hbm, qgain), (kgain_hbm, kgain),
+        (gscale_hbm, gscale), (uscale_hbm, uscale),
+    )
+    loads = [pltpu.make_async_copy(a, b, ld.at[5 + i]) for i, (a, b) in enumerate(pairs)]
+    for c in loads[2:5] + loads[:2] + loads[5:] + load_wq:
         c.start()
     load_kc.start()
     load_vc.start()
@@ -103,11 +110,14 @@
     for to in (across, ZP, ZM):
         pl.semaphore_signal(barrier, inc=1, device_id=to, device_id_type=MESH)
 
+    for c in loads:
+        c.wait()
+    turned = jnp.transpose(wdown[...])
     for s in range(4):
         piece = jnp.concatenate([wgate[:, HID * s : HID * s + HID], wup[:, HID * s : HID * s + HID]], axis=1)
         gu4[s] = piece[:, :384]
         dn4[s] = jnp.zeros((56, 256), jnp.int32)
-        dn4[s, 0:50, 0:160] = wdown[50 * s : 50 * s + 50, :]
+        dn4[s, 0:50, 0:160] = turned[50 * s : 50 * s + 50, :]
         dn4[s, 0:40, 160:176] = piece[:, 384:400]
     gub[0, pl.ds(mo(src * 40, 8), 40), :] = gu4[src]
     dnp[src] = dn4[src]
@@ -128,9 +138,11 @@
         at = pl.ds(mo(g * 512, 512), 512)
         v = (hid[:, at].astype(F32) * stage[:, 0:1] * vec[0:1, at]).astype(BF)
         v = dot(v, p512[...]).astype(BF)
-        w = wq[pl.ds(mo(g * 128, 128), 128), :]
+        w = wq[:, pl.ds(mo(g * 128, 128), 128)]
         for k in range(4):
-            acc = acc + dot(v[:, k * 128 : (k + 1) * 128], byte_of(w, k))
+            acc = acc + lax.dot_general(
+                v[:, k * 128 : (k + 1) * 128], byte_of(w, k), (((1,), (1,)), ((), ())), preferred_element_type=F32
+            )
         return acc
 
     load_wq[0].wait()
@@ -177,9 +189,12 @@
 
     lax.fori_loop(1, 16, start_b, 0)
     wo_side = (x + 1 + 2 * core) % 4
+    wo_rows = pl.ds(mo(core * 32, 32), 32)
     wo_copy = rcopy(
-        wout.at[:, pl.ds(mo((1 - xl) * HALF, 128), HALF)], wo_r, wos, wor, at_x(wo_side, core)
+        wout.at[wo_rows, pl.ds(mo((1 - xl) * HALF, 128), HALF)], wo_r.at[wo_rows, :], wos.at[0], wor.at[0],
+        at_x(wo_side, core),
     )
+    wo_share = rcopy(wo_r.at[wo_rows, :], wo_r.at[wo_rows, :], wos.at[1], wor.at[1], SIB)
     wo_copy.start()
     brecv[pl.ds(tp, 1)] = bsend[pl.ds(tp, 1)]
 
@@ -222,16 +237,15 @@
     def to_sib(slot):
         return rcopy(dnb.at[slot], dns.at[slot], ns.at[slot], nr.at[slot], SIB)
 
-    def hop(step):
-        for h in (xh, 1 - xh):
-            ring_wait(h, step)
+    def hop(stream, step):
+        h = xh if stream == 0 else 1 - xh
+        ring_wait(h, step)
+        if step < 4:
+            ring_start(h, step + 1)
+        if stream == 1:
+            to_sib(step).start()
             if step < 4:
-                ring_start(h, step + 1)
-        if step < 4:
-            to_sib(step).start()
-            to_sib(8 - step).start()
-        else:
-            to_sib(4).start()
+                to_sib(8 - step).start()
 
     def unpack_down(ref, slot, which):
         zz = (z + ZS - slot) % ZS
@@ -294,7 +308,6 @@
     assemble(1 - xh)
     ring_start(1 - xh, 1)
     to_sib(0).start()
-    unpack(0)
     load_kc.wait()
     load_vc.wait()
     half = lax.broadcasted_iota(jnp.int32, (8, HEAD), 1)
@@ -309,6 +322,8 @@
     stab = jnp.where(half < 64, -stab, stab)
 
     lax.fori_loop(1, 16, wait_b, 0)
+    wo_copy.wait_recv()
+    wo_share.start()
     lane = lax.broadcasted_iota(jnp.int32, (4, HEAD), 1)
     for p in range(8):
         even, odd = brecv[2 * p], brecv[2 * p + 1]
@@ -389,9 +404,11 @@
     lax.fori_loop(1, 16, start_h, 0)
     hrecv[pl.ds(mo(tp * 16, 16), 16), :] = hsend[y]
 
-    wo_copy.wait_recv()
+    hop(0, 1)
+    unpack(0)
+    wo_share.wait_recv()
     unpack_wo(wo_r, (1 - xl) * 256)
-    hop(1)
+    hop(1, 1)
 
     lax.fori_loop(1, 16, wait_h, 0)
     P128 = one_hot(128, 32, 32)
@@ -405,78 +422,68 @@
         zcat.append(dot(dot(pick, got).astype(BF), P128).astype(BF))
     zcat = jnp.concatenate(zcat, axis=1)
 
-    def part(yy):
-        return pl.ds(mo(32 * (yy // 4), 32), 32), pl.ds(mo(640 * (yy % 4), 128), 640)
+    def part(yy, s):
+        return pl.ds(mo(32 * (yy // 4) + 16 * s, 16), 16), pl.ds(mo(640 * (yy % 4), 128), 640)
 
     for cb in range(4):
         pm[:, cb * 640 : cb * 640 + 640] = dot(zcat, wo[:, cb * 640 : cb * 640 + 640]).astype(BF)
 
-    def r_copy(d):
+    def r_copy(d, s):
         to = (y + d) % YS
-        a, b = part(to)
-        return rcopy(pm.at[a, b], rs.at[y], rss.at[to], rsr.at[y], {"tp": xl * YS + to})
-
-    def wait_r(d, _):
+        a, b = part(to, s)
+        return rcopy(pm.at[a, b], rs.at[s, y], rss.at[s, to], rsr.at[s, y], {"tp": xl * YS + to})
+
+    def wait_r(d, s):
         frm = (y + d) % YS
-        a, b = part(frm)
-        rcopy(pm.at[a, b], rs.at[frm], rss.at[frm], rsr.at[frm], {"tp": xl * YS + frm}).wait_recv()
-        return 0
-
-    for d in NEAR[:0:-1]:
-        r_copy(d).start()
-    a, b = part(y)
-    rs[y] = pm[a, b]
+        a, b = part(frm, s)
+        rcopy(pm.at[a, b], rs.at[s, frm], rss.at[s, frm], rsr.at[s, frm], {"tp": xl * YS + frm}).wait_recv()
+
+    for s in (0, 1):
+        for d in NEAR[:0:-1]:
+            r_copy(d, s).start()
+        a, b = part(y, s)
+        rs[s, y] = pm[a, b]
     unpack(1)
     unpack(7)
     unpack_sib(0)
-    hop(2)
-
-    lax.fori_loop(1, YS, wait_r, 0)
-    mid = rs[0].astype(F32)
-    for i in range(1, YS):
-        mid = mid + rs[i].astype(F32)
-    cols = pl.ds(mo(xl * HALF + 640 * (y % 4), 128), 640)
-    mid = hid[a, cols].astype(F32) + mid * vec[2:3, cols]
-    X[pl.ds(mo(src * 64 + 32 * (y // 4), 32), 32), cols] = mid.astype(BF)
-
-    def blk(xx, cc, yy):
-        r0 = ((xx // 2) * 2 + cc) * 64 + 32 * (yy // 4)
+    hop(0, 2)
+
+    def blk(xx, cc, yy, s):
+        r0 = ((xx // 2) * 2 + cc) * 64 + 32 * (yy // 4) + 16 * s
         c0 = (xx % 2) * HALF + 640 * (yy % 4)
-        return X.at[pl.ds(mo(r0, 32), 32), pl.ds(mo(c0, 128), 640)]
-
-    def fy_copy(d):
+        return X.at[pl.ds(mo(r0, 16), 16), pl.ds(mo(c0, 128), 640)]
+
+    def fy_copy(d, s):
         to = (y + d) % YS
-        return rcopy(blk(x, core, y), blk(x, core, y), fys.at[to], fyr.at[y], {"tp": xl * YS + to})
-
-    for d in NEAR[1:]:
-        fy_copy(d).start()
-
-    def fx_copy(way, i):
-        b0 = blk(x, core, (y + i) % YS)
-        return rcopy(b0, b0, fxs.at[way, i], fxr.at[way, i], PLUS if way == 0 else MINUS)
-
-    def fx_in(way, i):
-        b0 = blk(xm if way == 0 else xp, core, (y + i) % YS)
-        return rcopy(b0, b0, fxs.at[way, i], fxr.at[way, i], MINUS if way == 0 else PLUS)
-
-    def fq_copy(i):
+        b0 = blk(x, core, y, s)
+        return rcopy(b0, b0, fys.at[s, to], fyr.at[s, y], {"tp": xl * YS + to})
+
+    def fx_copy(way, i, s):
+        b0 = blk(x, core, (y + i) % YS, s)
+        return rcopy(b0, b0, fxs.at[s, way, i], fxr.at[s, way, i], PLUS if way == 0 else MINUS)
+
+    def fx_in(way, i, s):
+        b0 = blk(xm if way == 0 else xp, core, (y + i) % YS, s)
+        return rcopy(b0, b0, fxs.at[s, way, i], fxr.at[s, way, i], MINUS if way == 0 else PLUS)
+
+    def fq_copy(i, s):
         way = i % 2
-        b0 = blk(xm if way == 0 else xp, core, (y + i) % YS)
-        return rcopy(b0, b0, fqs.at[i], fqr.at[i], PLUS if way == 0 else MINUS)
-
-    def fq_in(i):
-        b0 = blk(xo, core, (y + i) % YS)
-        return rcopy(b0, b0, fqs.at[i], fqr.at[i], MINUS if i % 2 == 0 else PLUS)
+        b0 = blk(xm if way == 0 else xp, core, (y + i) % YS, s)
+        return rcopy(b0, b0, fqs.at[s, i], fqr.at[s, i], PLUS if way == 0 else MINUS)
+
+    def fq_in(i, s):
+        b0 = blk(xo, core, (y + i) % YS, s)
+        return rcopy(b0, b0, fqs.at[s, i], fqr.at[s, i], MINUS if i % 2 == 0 else PLUS)
 
     froms = (x, xm, xp, xo)
 
-    def fs_copy(j, i):
-        b0 = blk(froms[j], core, (y + i) % YS)
-        return rcopy(b0, b0, fss.at[j, i], fsr.at[j, i], SIB)
-
-    def fs_in(j, i):
-        b0 = blk(froms[j], 1 - core, (y + i) % YS)
-        return rcopy(b0, b0, fss.at[j, i], fsr.at[j, i], SIB)
+    def fs_copy(j, i, s):
+        b0 = blk(froms[j], core, (y + i) % YS, s)
+        return rcopy(b0, b0, fss.at[s, j, i], fsr.at[s, j, i], SIB)
+
+    def fs_in(j, i, s):
+        b0 = blk(froms[j], 1 - core, (y + i) % YS, s)
+        return rcopy(b0, b0, fss.at[s, j, i], fsr.at[s, j, i], SIB)
 
     def gained(xx, cc):
         at = pl.ds(mo(((xx // 2) * 2 + cc) * 64, 64), 64)
@@ -492,48 +499,80 @@
                 xk[k, at, to] = v[:, k * 128 : (k + 1) * 128]
         ssq[xx % 2, at, :] = jnp.broadcast_to(total, (64, HEAD))
 
-    for n, i in enumerate(NEAR):
+    def onward(i, s):
+        fx_copy(0, i, s).start()
+        fx_copy(1, i, s).start()
+        fs_copy(0, i, s).start()
+
+    def mid(s):
+        for d in NEAR[1:]:
+            wait_r(d, s)
+        m = rs[s, 0].astype(F32)
+        for i in range(1, YS):
+            m = m + rs[s, i].astype(F32)
+        cols = pl.ds(mo(xl * HALF + 640 * (y % 4), 128), 640)
+        m = hid[pl.ds(mo(32 * (y // 4) + 16 * s, 16), 16), cols].astype(F32) + m * vec[2:3, cols]
+        X[pl.ds(mo(src * 64 + 32 * (y // 4) + 16 * s, 16), 16), cols] = m.astype(BF)
+        for d in NEAR[1:]:
+            fy_copy(d, s).start()
+        onward(0, s)
+
+    def from_y(i, s):
         yy = (y + i) % YS
-        if i:
-            b0 = blk(x, core, yy)
-            rcopy(b0, b0, fys.at[yy], fyr.at[yy], {"tp": xl * YS + yy}).wait_recv()
-        fx_copy(0, i).start()
-        fx_copy(1, i).start()
-        fs_copy(0, i).start()
-        if n == 3:
-            unpack(2)
-            unpack(6)
-            unpack_sib(1)
-            unpack_sib(7)
-            hop(3)
+        b0 = blk(x, core, yy, s)
+        rcopy(b0, b0, fys.at[s, yy], fyr.at[s, yy], {"tp": xl * YS + yy}).wait_recv()
+        onward(i, s)
+
+    def from_x(i, s):
+        fx_in(0, i, s).wait_recv()
+        fx_in(1, i, s).wait_recv()
+        fq_copy(i, s).start()
+        fs_copy(1, i, s).start()
+        fs_copy(2, i, s).start()
+
+    def from_sib(j):
+        for s in (0, 1):
+            for i in NEAR:
+                fs_in(j, i, s).wait_recv()
+        gained(froms[j], 1 - core)
+
+    mid(0)
+    hop(1, 2)
+    mid(1)
+    for i in NEAR[1:]:
+        from_y(i, 0)
+    hop(0, 3)
+    from_x(0, 0)
+    unpack(2)
+    unpack(6)
+    for i in NEAR[1:]:
+        from_y(i, 1)
+        from_x(i, 0)
+    hop(1, 3)
+    unpack_sib(1)
+    unpack_sib(7)
     gained(x, core)
     for i in NEAR:
-        fx_in(0, i).wait_recv()
-        fx_in(1, i).wait_recv()
-        fq_copy(i).start()
-        fs_copy(1, i).start()
-        fs_copy(2, i).start()
+        from_x(i, 1)
     gained(xm, core)
     gained(xp, core)
+    hop(0, 4)
+    hop(1, 4)
     unpack(3)
     unpack(5)
     unpack_sib(2)
     unpack_sib(6)
-    for i in NEAR:
-        fs_in(0, i).wait_recv()
-    gained(x, 1 - core)
-    hop(4)
+    for j in (0, 1, 2):
+        from_sib(j)
     unpack(4)
     unpack_sib(3)
     unpack_sib(5)
-    for i in NEAR:
-        fq_in(i).wait_recv()
-        fs_copy(3, i).start()
+    for s in (0, 1):
+        for i in NEAR:
+            fq_in(i, s).wait_recv()
+            fs_copy(3, i, s).start()
     gained(xo, core)
-    for j in (1, 2, 3):
-        for i in NEAR:
-            fs_in(j, i).wait_recv()
-        gained(froms[j], 1 - core)
+    from_sib(3)
     gsc[...] = jnp.zeros((8, 1024), F32)
     gsc[0:1, :800] = gscale[...][None, :]
     gsc[1:2, :800] = uscale[...][None, :]
@@ -575,14 +614,14 @@
             pd[:, at] = r.astype(BF)
             return 0
 
-        lax.fori_loop(0, 2, some, 0)
+        lax.fori_loop(0, 4, some, 0)
 
     sides = (PLUS, MINUS)
     nexts = (xp, xm)
 
     def slab(xx, q, w):
-        rows = pl.ds(mo((xx // 2) * 64, 64), 64)
-        return rows, pl.ds(mo((xx % 2) * HALF + q * 1280 + w * 640, 128), 640)
+        rows = pl.ds(mo((xx // 2) * 64 + q * 16, 16), 16)
+        return rows, pl.ds(mo((xx % 2) * HALF + w * 1280, 128), 1280)
 
     def pre_copy(q, w):
         a, b = slab(xo, q, w)
@@ -594,6 +633,14 @@
 
     def merge_copy(q, w):
         return rcopy(smerge.at[q, w], rmerge.at[q, w], xms.at[q, w], xmr.at[q, w], sides[w])
+
+    def pre_start(q):
+        for w in (0, 1):
+            pre_copy(q, w).start()
+
+    def plain_start(q):
+        for w in (0, 1):
+            plain_copy(q, w).start()
 
     def merge(q):
         for w in (0, 1):
@@ -605,51 +652,50 @@
     def window(yy):
         return pl.ds(mo(320 * yy - 64 * (yy % 2), 128), 384)
 
+    def y_copy(d, q):
+        to = (y + d) % YS
+        at = pl.ds(q * 16, 16)
+        return rcopy(u.at[at, window(to)], yr.at[y, at, :], yss.at[q, to], ysr.at[q, y], {"tp": xl * YS + to})
+
+    def y_in(d, q):
+        frm = (y + d) % YS
+        at = pl.ds(q * 16, 16)
+        return rcopy(u.at[at, window(frm)], yr.at[frm, at, :], yss.at[q, frm], ysr.at[q, frm], {"tp": xl * YS + frm})
+
     def finish(q):
+        at = slice(q * 16, q * 16 + 16)
         for w in (0, 1):
             plain_copy(q, w).wait_recv()
         for w in (0, 1):
             merge_copy(q, w).wait_recv()
             a, b = slab(x, q, w)
             v = pd[a, b].astype(F32) + rplain[q, 1 - w].astype(F32) + rmerge[q, w].astype(F32)
-            u[:, q * 1280 + w * 640 : q * 1280 + w * 640 + 640] = v.astype(BF)
-
-    def y_copy(to):
-        return rcopy(u.at[:, window(to)], yr.at[y], yss.at[to], ysr.at[y], {"tp": xl * YS + to})
-
-    def y_sends(q):
-        for i in range(4):
-            to = 4 * q + i
-
-            @pl.when(to != y)
-            def _():
-                y_copy(to).start()
-
-            @pl.when(to == y)
-            def _():
-                yr[y] = u[:, window(to)]
+            u[at, w * 1280 : w * 1280 + 1280] = v.astype(BF)
+        for d in NEAR[:0:-1]:
+            y_copy(d, q).start()
+        yr[y, at, :] = u[at, window(y)]
 
     down(xl * HALF)
-    for w in (0, 1):
-        pre_copy(0, w).start()
+    pre_start(0)
+    pre_start(1)
     down((1 - xl) * HALF)
-    for w in (0, 1):
-        plain_copy(0, w).start()
-    down(xl * HALF + 1280)
-    for w in (0, 1):
-        pre_copy(1, w).start()
-    down((1 - xl) * HALF + 1280)
-    for w in (0, 1):
-        plain_copy(1, w).start()
+    plain_start(0)
     merge(0)
+    pre_start(2)
+    plain_start(1)
     merge(1)
+    pre_start(3)
+    plain_start(2)
     finish(0)
-    y_sends(0)
+    merge(2)
+    plain_start(3)
     finish(1)
-    y_sends(1)
-    for d in NEAR[1:]:
-        frm = (y + d) % YS
-        rcopy(u.at[:, window(frm)], yr.at[frm], yss.at[frm], ysr.at[frm], {"tp": xl * YS + frm}).wait_recv()
+    merge(3)
+    finish(2)
+    finish(3)
+    for q in range(4):
+        for d in NEAR[1:]:
+            y_in(d, q).wait_recv()
     last = yr[0].astype(F32)
     for i in range(1, YS):
         last = last + yr[i].astype(F32)
@@ -662,6 +708,7 @@
         w1_gu(d).wait_send()
         w1_dn(d).wait_send()
     wo_copy.wait_send()
+    wo_share.wait_send()
     for h in (0, 1):
         for step in (1, 2, 3, 4):
             for way in (0, 1):
@@ -675,23 +722,23 @@
         h_copy(d).wait_send()
         return 0
 
-    def sent_y(d, _):
-        r_copy(d).wait_send()
-        fy_copy(d).wait_send()
-        y_copy((y + d) % YS).wait_send()
-        return 0
-
     lax.fori_loop(1, 16, sent_tp, 0)
-    lax.fori_loop(1, YS, sent_y, 0)
-    for i in range(YS):
-        fx_copy(0, i).wait_send()
-        fx_copy(1, i).wait_send()
-        fq_copy(i).wait_send()
-        for j in range(4):
-            fs_copy(j, i).wait_send()
+    for d in NEAR[1:]:
+        for s in (0, 1):
+            r_copy(d, s).wait_send()
+            fy_copy(d, s).wait_send()
+        for q in range(4):
+            y_copy(d, q).wait_send()
+    for s in (0, 1):
+        for i in range(YS):
+            fx_copy(0, i, s).wait_send()
+            fx_copy(1, i, s).wait_send()
+            fq_copy(i, s).wait_send()
+            for j in range(4):
+                fs_copy(j, i, s).wait_send()
     for w in (0, 1):
         ac_copy(w).wait_send()
-        for q in (0, 1):
+        for q in range(4):
             pre_copy(q, w).wait_send()
             plain_copy(q, w).wait_send()
             merge_copy(q, w).wait_send()
@@ -704,26 +751,26 @@
     V, S = pltpu.VMEM, pltpu.SemaphoreType.DMA
     I32 = jnp.int32
     scratch = [
-        V((1280, 320), I32), V((4, 128, 512), BF), V((4, 128, 512), BF), V((64, HALF), I32), V((512, 512), BF),
+        V((ROWS, D), BF), V((D,), F32), V((320,), F32), V((HEAD,), F32), V((HEAD,), F32), V((D,), F32), V((D,), F32),
+        V((40, 800), I32), V((40, 800), I32), V((800,), F32), V((800,), F32), V((160, HID), I32), V((D,), F32),
+        V((320, 1280), I32), V((4, 128, 512), BF), V((4, 128, 512), BF), V((64, HALF), I32), V((512, 512), BF),
         V((8, D), F32), V((8, 1024), F32),
         V((ROWS, 384), F32), V((4, 40, 384), I32), V((4, 56, 256), I32),
         V((16, 4, 384), F32), V((16, 4, 384), F32), V((160, HEAD), F32), V((32, HEAD), F32),
         V((YS, 16, HEAD), BF), V((256, HEAD), BF), V((64, HALF), I32), V((512, HALF), BF), V((ROWS, HALF), BF),
-        V((YS, 32, 640), BF), V((ALL, D), BF), V((4, ALL, 1280), BF), V((2, ALL, HEAD), F32),
+        V((2, YS, 16, 640), BF), V((ALL, D), BF), V((4, ALL, 1280), BF), V((2, ALL, HEAD), F32),
         V((ZS, 160, 384), I32), V((4, 56, 256), I32), V((ZS, 2, 56, 384), I32), V((ZS, 2, 56, 384), I32),
         V((4, 1280, 512), BF), V((2, 256, D), BF), V((2, ROWS, PAD), BF), V((2 * ROWS, D), BF),
-        V((2, 2, ROWS, 640), BF), V((2, 2, ROWS, 640), BF), V((2, 2, ROWS, 640), BF), V((2, 2, ROWS, 640), BF),
+        V((4, 2, 16, 1280), BF), V((4, 2, 16, 1280), BF), V((4, 2, 16, 1280), BF), V((4, 2, 16, 1280), BF),
         V((ROWS, HALF), BF), V((YS, ROWS, 384), BF),
-        S((5,)), S((2, 4)), S((2, 4)), S, S, S((2, 2, 4, 2)), S((2, 2, 4, 2)), S((8,)), S((8,)),
+        S((18,)), S((2, 4)), S((2, 4)), S((2,)), S((2,)), S((2, 2, 4, 2)), S((2, 2, 4, 2)), S((8,)), S((8,)),
         S((16,)), S((16,)), S((16,)), S((16,)),
-        S((8,)), S((8,)), S((8,)), S((8,)), S((2, 8)), S((2, 8)), S((8,)), S((8,)), S((4, 8)), S((4, 8)),
-        S((2,)), S((2,)), S((2, 2)), S((2, 2)), S((2, 2)), S((2, 2)), S((2, 2)), S((2, 2)), S((8,)), S((8,)),
+        S((2, 8)), S((2, 8)), S((2, 8)), S((2, 8)), S((2, 2, 8)), S((2, 2, 8)), S((2, 8)), S((2, 8)), S((2, 4, 8)), S((2, 4, 8)),
+        S((2,)), S((2,)), S((4, 2)), S((4, 2)), S((4, 2)), S((4, 2)), S((4, 2)), S((4, 2)), S((4, 8)), S((4, 8)),
     ]
     vmem = pl.BlockSpec(memory_space=pltpu.VMEM)
     far = pl.BlockSpec(memory_space=pl.ANY)
-    specs = [vmem] * 18
-    for i in (2, 6, 7, 9):
-        specs[i] = far
+    specs = [far] * 18
     specs[8] = pl.BlockSpec(memory_space=pltpu.SMEM)
     return pl.pallas_call(
         kernel,
@@ -736,8 +783,8 @@
         ),
         name="layer",
     )(
-        hidden_in, attn_gain, w_qkv, qkv_scale, q_gain, k_gain, key_cache, value_cache, lengths, w_out, out_scale,
-        mlp_gain, w_gate, w_up, gate_scale, up_scale, w_down, down_scale,
+        hidden_in, attn_gain, w_qkv.T, qkv_scale, q_gain, k_gain, key_cache, value_cache, lengths, w_out, out_scale,
+        mlp_gain, w_gate, w_up, gate_scale, up_scale, w_down.T, down_scale,
     )
 
 

time: 101 us -> 93.4 us (0.925)
  the two profiles are of different devices: /device:TPU:56 before, /device:TPU:6 now
where the time goes in v2:
time: 93.4 us; the launch traced here: 93 us
  Pallas kernels  91.5 us (98%)
  local copies, waits for them, and re-layouts  1.42 us (2%)
    pallas_call x1, Pallas kernels, local(): pl.pallas_call(kernel, out_shape=jax.ShapeDtypeStruct((ROWS, 320), BF), i...  91.5 us

profile of v2, /device:TPU:6, one launch (start us, length us, event | category | flops | bytes accessed | tf_op | source)
XLA Modules:
  0.0 93.0 jit_solution(5924086136877697806)
XLA Ops:
  0.0 91.5 %layer.1 = bf16[64,320]{1,0:T(8,128)(2,1)} custom-call(bf16[64,5120]{1,0:T(8,128)(2,1)} %hid_hbm.1, f32[5120]{0:T(1024)} %again_hbm.1, s32[320,1280]{1,0:T(8,128)} %bitcast.2, f32[320]{0:T(512)} %qscale_hbm.1, f32[128]{0:T(128)} %qgain_hbm.1, f32[128]{0:T(128)} %kgain_hbm.1, bf16[1,4,128,512]{3,2,1,0:T(8,128)(2,1)} %kc_hbm.1, ...), custom_call_target="tpu_custom_call" | custom-call | tf_op jit(solution)/shard_map/layer/pallas_call | solution.py:775
  91.5 1.4 %copy.20 = bf16[64,320]{1,0:T(8,128)(2,1)} copy(bf16[64,320]{1,0:T(8,128)(2,1)} %layer.1) | data formatting | bytes 81920

commit v3 on v2

--- a/solution.py
+++ b/solution.py
@@ -51,7 +51,7 @@
     wgate_hbm, wup_hbm, gscale_hbm, uscale_hbm, wdown_hbm, dscale_hbm,
     out,
     hid, again, qscale, qgain, kgain, oscale, mgain, wgate, wup, gscale, uscale, wdown, dscale,
-    wq, kc, vc, woh, p512, vec, gsc, stage, gu4, dn4, bsend, brecv, qs, vs, hsend, hrecv, wo_r, wo, pm, rs, X, xk, ssq,
+    wq, kc, vc, woh, p512, p128, p256, picks, half_down, vec, gsc, stage, gu4, dn4, bsend, brecv, qs, vs, hsend, hrecv, wo_r, wo, pm, rs, X, xk, ssq,
     gub, dnp, dnb, dns, wg, wd, actr, pd, pre, smerge, rplain, rmerge, u, yr,
     ld, w1s, w1r, wos, wor, zs, zr, ns, nr, bs, br, hs, hr, rss, rsr, fys, fyr, fxs, fxr, fqs, fqr, fss, fsr,
     acs, acr, xps, xpr, xas, xar, xms, xmr, yss, ysr,
@@ -132,21 +132,11 @@
         v = hid[:, g * 512 : (g + 1) * 512].astype(F32)
         total = total + jnp.sum(v * v, axis=1, keepdims=True)
     rms = lax.rsqrt(total * (1.0 / D) + EPS)
-    stage[...] = jnp.broadcast_to(rms, (ROWS, 384))
-
-    def qkv_group(g, acc):
-        at = pl.ds(mo(g * 512, 512), 512)
-        v = (hid[:, at].astype(F32) * stage[:, 0:1] * vec[0:1, at]).astype(BF)
-        v = dot(v, p512[...]).astype(BF)
-        w = wq[:, pl.ds(mo(g * 128, 128), 128)]
-        for k in range(4):
-            acc = acc + lax.dot_general(
-                v[:, k * 128 : (k + 1) * 128], byte_of(w, k), (((1,), (1,)), ((), ())), preferred_element_type=F32
-            )
-        return acc
-
-    load_wq[0].wait()
-    acc = lax.fori_loop(0, 5, qkv_group, jnp.zeros((ROWS, 320), F32))
+
+    for g in range(10):
+        at = slice(g * 512, g * 512 + 512)
+        v = (hid[:, at].astype(F32) * rms * vec[0:1, at]).astype(BF)
+        xk[:ROWS, at] = dot(v, p512[...]).astype(BF)
     pl.semaphore_wait(barrier, 21)
 
     def w1_gu(d):
@@ -163,8 +153,18 @@
         w1_gu(d).start()
         w1_dn(d).start()
 
-    load_wq[1].wait()
-    acc = lax.fori_loop(5, 10, qkv_group, acc)
+    acc = jnp.zeros((ROWS, 320), F32)
+    for c in load_wq:
+        c.wait()
+    for g in range(10):
+        w = wq[:, g * 128 : g * 128 + 128]
+        for k in (0, 2):
+            acc = acc + lax.dot_general(
+                xk[:ROWS, g * 512 + k * 128 : g * 512 + k * 128 + 256],
+                jnp.concatenate([byte_of(w, k), byte_of(w, k + 1)], axis=1),
+                (((1,), (1,)), ((), ())),
+                preferred_element_type=F32,
+            )
     qkv = (acc * qscale[...][None, :]).astype(BF).astype(F32)
     stage[...] = jnp.zeros((ROWS, 384), F32)
     stage[:, :320] = qkv
@@ -261,7 +261,7 @@
         def rows(i, _):
             w = gub[slot, pl.ds(mo(i * 32, 32), 32), :]
             for k in range(4):
-                wg[k, pl.ds(mo(zz * 160 + i * 32, 32), 32), 0:384] = byte_of(w, k)
+                wg[pl.ds(mo(k * 1280 + zz * 160 + i * 32, 32), 32), 0:384] = byte_of(w, k)
             return 0
 
         lax.fori_loop(0, 5, rows, 0)
@@ -272,7 +272,7 @@
             tails.append(jnp.where(lane40 < 16, t, 0))
         tails = jnp.concatenate(tails, axis=0)
         for k in range(4):
-            wg[k, pl.ds(mo(zz * 160, 32), 160), 384:512] = byte_of(tails, k)
+            wg[pl.ds(mo(k * 1280 + zz * 160, 32), 160), 384:512] = byte_of(tails, k)
         unpack_down(dnb, slot, 0)
 
     def unpack_sib(slot):
@@ -321,6 +321,13 @@
     stab = jnp.sin(angle)
     stab = jnp.where(half < 64, -stab, stab)
 
+    p128[...] = one_hot(128, 32, 32)
+    p256[...] = one_hot(PAD, HID // 4, 64)
+    t = lax.broadcasted_iota(jnp.int32, (ROWS, 256), 0)
+    c = lax.broadcasted_iota(jnp.int32, (ROWS, 256), 1)
+    for hl in range(4):
+        want = jnp.right_shift(t, 2) * 16 + hl * 4 + jnp.bitwise_and(t, 3)
+        picks[hl] = jnp.where(c == want, 1.0, 0.0).astype(BF)
     lax.fori_loop(1, 16, wait_b, 0)
     wo_copy.wait_recv()
     wo_share.start()
@@ -411,15 +418,8 @@
     hop(1, 1)
 
     lax.fori_loop(1, 16, wait_h, 0)
-    P128 = one_hot(128, 32, 32)
     got = hrecv[...]
-    t = lax.broadcasted_iota(jnp.int32, (ROWS, 256), 0)
-    c = lax.broadcasted_iota(jnp.int32, (ROWS, 256), 1)
-    zcat = []
-    for hl in range(4):
-        want = jnp.right_shift(t, 2) * 16 + hl * 4 + jnp.bitwise_and(t, 3)
-        pick = jnp.where(c == want, 1.0, 0.0).astype(BF)
-        zcat.append(dot(dot(pick, got).astype(BF), P128).astype(BF))
+    zcat = [dot(dot(picks[hl], got).astype(BF), p128[...]).astype(BF) for hl in range(4)]
     zcat = jnp.concatenate(zcat, axis=1)
 
     def part(yy, s):
@@ -453,10 +453,11 @@
         c0 = (xx % 2) * HALF + 640 * (yy % 4)
         return X.at[pl.ds(mo(r0, 16), 16), pl.ds(mo(c0, 128), 640)]
 
-    def fy_copy(d, s):
-        to = (y + d) % YS
-        b0 = blk(x, core, y, s)
-        return rcopy(b0, b0, fys.at[s, to], fyr.at[s, y], {"tp": xl * YS + to})
+    def fy_copy(n, s):
+        i, hop_by = ((0, 1), (0, 7), (0, 2), (0, 6), (6, 1), (2, 7), (6, 2) if s == 0 else (2, 6))[n]
+        yy, to = (y + i) % YS, (y + hop_by) % YS
+        b0 = blk(x, core, yy, s)
+        return rcopy(b0, b0, fys.at[s, n], fyr.at[s, yy], {"tp": xl * YS + to})
 
     def fx_copy(way, i, s):
         b0 = blk(x, core, (y + i) % YS, s)
@@ -494,9 +495,9 @@
             v = X[at, cs].astype(F32)
             total = total + jnp.sum(v * v, axis=1, keepdims=True)
             v = dot((v * vec[1:2, cs]).astype(BF), p512[...]).astype(BF)
-            to = pl.ds(mo((xx % 2) * 640 + g * 128, 128), 128)
             for k in range(4):
-                xk[k, at, to] = v[:, k * 128 : (k + 1) * 128]
+                to = pl.ds(mo(k * 1280 + (xx % 2) * 640 + g * 128, 128), 128)
+                xk[at, to] = v[:, k * 128 : (k + 1) * 128]
         ssq[xx % 2, at, :] = jnp.broadcast_to(total, (64, HEAD))
 
     def onward(i, s):
@@ -513,14 +514,18 @@
         cols = pl.ds(mo(xl * HALF + 640 * (y % 4), 128), 640)
         m = hid[pl.ds(mo(32 * (y // 4) + 16 * s, 16), 16), cols].astype(F32) + m * vec[2:3, cols]
         X[pl.ds(mo(src * 64 + 32 * (y // 4) + 16 * s, 16), 16), cols] = m.astype(BF)
-        for d in NEAR[1:]:
-            fy_copy(d, s).start()
+        for n in range(4):
+            fy_copy(n, s).start()
         onward(0, s)
 
     def from_y(i, s):
         yy = (y + i) % YS
         b0 = blk(x, core, yy, s)
         rcopy(b0, b0, fys.at[s, yy], fyr.at[s, yy], {"tp": xl * YS + yy}).wait_recv()
+        if i in (2, 6):
+            fy_copy(4 if i == 6 else 5, s).start()
+            if i == (6 if s == 0 else 2):
+                fy_copy(6, s).start()
         onward(i, s)
 
     def from_x(i, s):
@@ -541,37 +546,37 @@
     mid(1)
     for i in NEAR[1:]:
         from_y(i, 0)
+    from_x(0, 0)
     hop(0, 3)
-    from_x(0, 0)
     unpack(2)
     unpack(6)
     for i in NEAR[1:]:
         from_y(i, 1)
         from_x(i, 0)
-    hop(1, 3)
-    unpack_sib(1)
-    unpack_sib(7)
     gained(x, core)
     for i in NEAR:
         from_x(i, 1)
+    hop(1, 3)
     gained(xm, core)
     gained(xp, core)
-    hop(0, 4)
-    hop(1, 4)
-    unpack(3)
-    unpack(5)
-    unpack_sib(2)
-    unpack_sib(6)
-    for j in (0, 1, 2):
-        from_sib(j)
-    unpack(4)
-    unpack_sib(3)
-    unpack_sib(5)
     for s in (0, 1):
         for i in NEAR:
             fq_in(i, s).wait_recv()
             fs_copy(3, i, s).start()
     gained(xo, core)
+    unpack(3)
+    unpack(5)
+    unpack_sib(1)
+    unpack_sib(7)
+    unpack_sib(2)
+    unpack_sib(6)
+    for j in (0, 1, 2):
+        from_sib(j)
+    hop(0, 4)
+    hop(1, 4)
+    unpack(4)
+    unpack_sib(3)
+    unpack_sib(5)
     from_sib(3)
     gsc[...] = jnp.zeros((8, 1024), F32)
     gsc[0:1, :800] = gscale[...][None, :]
@@ -580,41 +585,44 @@
     mine = shifted
     for s in range(1, 4):
         mine = jnp.where(src == s, pltpu.roll(shifted, 1024 - HID * s, 1), mine)
-    both = dot(xk[0], wg[0])
-    for k in range(1, 4):
-        both = both + dot(xk[k], wg[k])
+    both = dot(xk[...], wg[...])
     rms = lax.rsqrt((ssq[0, :, 0:1] + ssq[1, :, 0:1]) * (1.0 / D) + EPS)
     gate = both[:, :PAD] * rms * mine[0:1, :PAD]
     up = pltpu.roll(both, 512 - HID, 1)[:, :PAD] * rms * mine[1:2, :PAD]
     used = lax.broadcasted_iota(jnp.int32, (1, PAD), 1) < HID
     act = jnp.where(used, gate / (1.0 + jnp.exp(-gate)) * up, 0.0).astype(BF)
-    act = dot(act, one_hot(PAD, HID // 4, 64)).astype(BF)
-    xk[0, :, :PAD] = act
+    act = dot(act, p256[...]).astype(BF)
+    xk[:, :PAD] = act
 
     def act_rows(h, cc):
         return pl.ds(mo((h * 2 + cc) * 64, 64), 64)
 
     def ac_copy(h):
-        return rcopy(xk.at[0, act_rows(h, 1 - core), 0:PAD], actr.at[h], acs.at[h], acr.at[h], SIB)
+        return rcopy(xk.at[act_rows(h, 1 - core), 0:PAD], actr.at[h], acs.at[h], acr.at[h], SIB)
 
     for h in (0, 1):
         ac_copy(h).start()
     unpack_sib(4)
+    own_act = jnp.concatenate([xk[act_rows(0, core), 0:PAD], xk[act_rows(1, core), 0:PAD]], axis=0)
+
+    def first(n, _):
+        half_down[:, pl.ds(mo(n * 640, 128), 640)] = dot(own_act, wd[0, :, pl.ds(mo(xl * HALF + n * 640, 128), 640)])
+        return 0
+
+    lax.fori_loop(0, 4, first, 0)
     for h in (0, 1):
         ac_copy(h).wait_recv()
-    lhs = [
-        jnp.concatenate([xk[0, act_rows(0, core), 0:PAD], xk[0, act_rows(1, core), 0:PAD]], axis=0),
-        jnp.concatenate([actr[0], actr[1]], axis=0),
-    ]
-
-    def down(c0):
-        def some(n, _):
-            at = pl.ds(mo(c0 + n * 640, 128), 640)
-            r = dot(lhs[0], wd[0, :, at]) + dot(lhs[1], wd[1, :, at])
-            pd[:, at] = r.astype(BF)
-            return 0
-
-        lax.fori_loop(0, 4, some, 0)
+    sib_act = jnp.concatenate([actr[0], actr[1]], axis=0)
+
+    def second(n, _):
+        at = pl.ds(mo(xl * HALF + n * 640, 128), 640)
+        pd[:, at] = (half_down[:, pl.ds(mo(n * 640, 128), 640)] + dot(sib_act, wd[1, :, at])).astype(BF)
+        return 0
+
+    def other(n, _):
+        at = pl.ds(mo((1 - xl) * HALF + n * 640, 128), 640)
+        pd[:, at] = (dot(own_act, wd[0, :, at]) + dot(sib_act, wd[1, :, at])).astype(BF)
+        return 0
 
     sides = (PLUS, MINUS)
     nexts = (xp, xm)
@@ -675,10 +683,10 @@
             y_copy(d, q).start()
         yr[y, at, :] = u[at, window(y)]
 
-    down(xl * HALF)
+    lax.fori_loop(0, 4, second, 0)
     pre_start(0)
     pre_start(1)
-    down((1 - xl) * HALF)
+    lax.fori_loop(0, 4, other, 0)
     plain_start(0)
     merge(0)
     pre_start(2)
@@ -693,17 +701,6 @@
     merge(3)
     finish(2)
     finish(3)
-    for q in range(4):
-        for d in NEAR[1:]:
-            y_in(d, q).wait_recv()
-    last = yr[0].astype(F32)
-    for i in range(1, YS):
-        last = last + yr[i].astype(F32)
-    at = pl.ds(mo(xl * HALF + 320 * y - 64 * (y % 2), 128), 384)
-    last = X[pl.ds(mo(src * 64, 64), 64), at].astype(F32) + last * vec[3:4, at]
-    last = jnp.where(odd_y, pltpu.roll(last, 320, 1), last)
-    out[...] = last[:, :320].astype(BF)
-
     for d in (1, 2, 3):
         w1_gu(d).wait_send()
         w1_dn(d).wait_send()
@@ -726,10 +723,9 @@
     for d in NEAR[1:]:
         for s in (0, 1):
             r_copy(d, s).wait_send()
-            fy_copy(d, s).wait_send()
-        for q in range(4):
-            y_copy(d, q).wait_send()
     for s in (0, 1):
+        for n in range(7):
+            fy_copy(n, s).wait_send()
         for i in range(YS):
             fx_copy(0, i, s).wait_send()
             fx_copy(1, i, s).wait_send()
@@ -742,6 +738,20 @@
             pre_copy(q, w).wait_send()
             plain_copy(q, w).wait_send()
             merge_copy(q, w).wait_send()
+    for q in range(4):
+        for d in NEAR[1:]:
+            y_in(d, q).wait_recv()
+    last = yr[0].astype(F32)
+    for i in range(1, YS):
+        last = last + yr[i].astype(F32)
+    at = pl.ds(mo(xl * HALF + 320 * y - 64 * (y % 2), 128), 384)
+    last = X[pl.ds(mo(src * 64, 64), 64), at].astype(F32) + last * vec[3:4, at]
+    last = jnp.where(odd_y, pltpu.roll(last, 320, 1), last)
+    out[...] = last[:, :320].astype(BF)
+
+    for q in range(4):
+        for d in NEAR[1:]:
+            y_copy(d, q).wait_send()
 
 
 def local(
@@ -754,13 +764,14 @@
         V((ROWS, D), BF), V((D,), F32), V((320,), F32), V((HEAD,), F32), V((HEAD,), F32), V((D,), F32), V((D,), F32),
         V((40, 800), I32), V((40, 800), I32), V((800,), F32), V((800,), F32), V((160, HID), I32), V((D,), F32),
         V((320, 1280), I32), V((4, 128, 512), BF), V((4, 128, 512), BF), V((64, HALF), I32), V((512, 512), BF),
+        V((HEAD, HEAD), BF), V((PAD, PAD), BF), V((4, ROWS, 256), BF), V((2 * ROWS, HALF), F32),
         V((8, D), F32), V((8, 1024), F32),
         V((ROWS, 384), F32), V((4, 40, 384), I32), V((4, 56, 256), I32),
         V((16, 4, 384), F32), V((16, 4, 384), F32), V((160, HEAD), F32), V((32, HEAD), F32),
         V((YS, 16, HEAD), BF), V((256, HEAD), BF), V((64, HALF), I32), V((512, HALF), BF), V((ROWS, HALF), BF),
-        V((2, YS, 16, 640), BF), V((ALL, D), BF), V((4, ALL, 1280), BF), V((2, ALL, HEAD), F32),
+        V((2, YS, 16, 640), BF), V((ALL, D), BF), V((ALL, D), BF), V((2, ALL, HEAD), F32),
         V((ZS, 160, 384), I32), V((4, 56, 256), I32), V((ZS, 2, 56, 384), I32), V((ZS, 2, 56, 384), I32),
-        V((4, 1280, 512), BF), V((2, 256, D), BF), V((2, ROWS, PAD), BF), V((2 * ROWS, D), BF),
+        V((D, 512), BF), V((2, 256, D), BF), V((2, ROWS, PAD), BF), V((2 * ROWS, D), BF),
         V((4, 2, 16, 1280), BF), V((4, 2, 16, 1280), BF), V((4, 2, 16, 1280), BF), V((4, 2, 16, 1280), BF),
         V((ROWS, HALF), BF), V((YS, ROWS, 384), BF),
         S((18,)), S((2, 4)), S((2, 4)), S((2,)), S((2,)), S((2, 2, 4, 2)), S((2, 2, 4, 2)), S((8,)), S((8,)),

time: 93.4 us -> 94.7 us (1.014)
  Pallas kernels: 91.5 us -> 93.1 us
    pallas_call x1, Pallas kernels: 91.5 us -> 93.1 us  [local(): pl.pallas_call(kernel, out_shape=jax.ShapeDtypeStruct((ROWS, 320), BF), i...]
where the time goes in v3:
time: 94.7 us; the launch traced here: 94.5 us
  Pallas kernels  93.1 us (98%)
  local copies, waits for them, and re-layouts  1.42 us (1%)
    pallas_call x1, Pallas kernels, local(): pl.pallas_call(kernel, out_shape=jax.ShapeDtypeStruct((ROWS, 320), BF), i...  93.1 us

profile of v3, /device:TPU:6, one launch (start us, length us, event | category | flops | bytes accessed | tf_op | source)
XLA Modules:
  0.0 94.5 jit_solution(7091628119472887071)
XLA Ops:
  0.0 93.1 %layer.1 = bf16[64,320]{1,0:T(8,128)(2,1)} custom-call(bf16[64,5120]{1,0:T(8,128)(2,1)} %hid_hbm.1, f32[5120]{0:T(1024)} %again_hbm.1, s32[320,1280]{1,0:T(8,128)} %bitcast.2, f32[320]{0:T(512)} %qscale_hbm.1, f32[128]{0:T(128)} %qgain_hbm.1, f32[128]{0:T(128)} %kgain_hbm.1, bf16[1,4,128,512]{3,2,1,0:T(8,128)(2,1)} %kc_hbm.1, ...), custom_call_target="tpu_custom_call" | custom-call | tf_op jit(solution)/shard_map/layer/pallas_call | solution.py:786
  93.1 1.4 %copy.20 = bf16[64,320]{1,0:T(8,128)(2,1)} copy(bf16[64,320]{1,0:T(8,128)(2,1)} %layer.1) | data formatting | bytes 81920

commit v4 on v3

--- a/solution.py
+++ b/solution.py
@@ -329,8 +329,6 @@
         want = jnp.right_shift(t, 2) * 16 + hl * 4 + jnp.bitwise_and(t, 3)
         picks[hl] = jnp.where(c == want, 1.0, 0.0).astype(BF)
     lax.fori_loop(1, 16, wait_b, 0)
-    wo_copy.wait_recv()
-    wo_share.start()
     lane = lax.broadcasted_iota(jnp.int32, (4, HEAD), 1)
     for p in range(8):
         even, odd = brecv[2 * p], brecv[2 * p + 1]
@@ -412,10 +410,11 @@
     hrecv[pl.ds(mo(tp * 16, 16), 16), :] = hsend[y]
 
     hop(0, 1)
+    wo_copy.wait_recv()
+    wo_share.start()
     unpack(0)
     wo_share.wait_recv()
     unpack_wo(wo_r, (1 - xl) * 256)
-    hop(1, 1)
 
     lax.fori_loop(1, 16, wait_h, 0)
     got = hrecv[...]
@@ -443,21 +442,18 @@
             r_copy(d, s).start()
         a, b = part(y, s)
         rs[s, y] = pm[a, b]
-    unpack(1)
-    unpack(7)
     unpack_sib(0)
-    hop(0, 2)
+    hop(1, 1)
 
     def blk(xx, cc, yy, s):
         r0 = ((xx // 2) * 2 + cc) * 64 + 32 * (yy // 4) + 16 * s
         c0 = (xx % 2) * HALF + 640 * (yy % 4)
         return X.at[pl.ds(mo(r0, 16), 16), pl.ds(mo(c0, 128), 640)]
 
-    def fy_copy(n, s):
-        i, hop_by = ((0, 1), (0, 7), (0, 2), (0, 6), (6, 1), (2, 7), (6, 2) if s == 0 else (2, 6))[n]
-        yy, to = (y + i) % YS, (y + hop_by) % YS
-        b0 = blk(x, core, yy, s)
-        return rcopy(b0, b0, fys.at[s, n], fyr.at[s, yy], {"tp": xl * YS + to})
+    def fy_copy(d, s):
+        to = (y + d) % YS
+        b0 = blk(x, core, y, s)
+        return rcopy(b0, b0, fys.at[s, to], fyr.at[s, y], {"tp": xl * YS + to})
 
     def fx_copy(way, i, s):
         b0 = blk(x, core, (y + i) % YS, s)
@@ -486,19 +482,21 @@
         b0 = blk(froms[j], 1 - core, (y + i) % YS, s)
         return rcopy(b0, b0, fss.at[s, j, i], fsr.at[s, j, i], SIB)
 
-    def gained(xx, cc):
-        at = pl.ds(mo(((xx // 2) * 2 + cc) * 64, 64), 64)
-        total = jnp.zeros((64, 1), F32)
+    def gained(*slabs):
+        side = slabs[0][0] % 2
+        rows = [pl.ds(mo(((xx // 2) * 2 + cc) * 64, 64), 64) for xx, cc in slabs]
+        total = jnp.zeros((64 * len(rows), 1), F32)
         for g in range(5):
-            c0 = (xx % 2) * HALF + g * 512
-            cs = pl.ds(mo(c0, 128), 512)
-            v = X[at, cs].astype(F32)
+            cs = pl.ds(mo(side * HALF + g * 512, 128), 512)
+            v = jnp.concatenate([X[at, cs] for at in rows], axis=0).astype(F32)
             total = total + jnp.sum(v * v, axis=1, keepdims=True)
             v = dot((v * vec[1:2, cs]).astype(BF), p512[...]).astype(BF)
             for k in range(4):
-                to = pl.ds(mo(k * 1280 + (xx % 2) * 640 + g * 128, 128), 128)
-                xk[at, to] = v[:, k * 128 : (k + 1) * 128]
-        ssq[xx % 2, at, :] = jnp.broadcast_to(total, (64, HEAD))
+                to = pl.ds(mo(k * 1280 + side * 640 + g * 128, 128), 128)
+                for n, at in enumerate(rows):
+                    xk[at, to] = v[n * 64 : n * 64 + 64, k * 128 : (k + 1) * 128]
+        for n, at in enumerate(rows):
+            ssq[side, at, :] = jnp.broadcast_to(total[n * 64 : n * 64 + 64], (64, HEAD))
 
     def onward(i, s):
         fx_copy(0, i, s).start()
@@ -514,18 +512,14 @@
         cols = pl.ds(mo(xl * HALF + 640 * (y % 4), 128), 640)
         m = hid[pl.ds(mo(32 * (y // 4) + 16 * s, 16), 16), cols].astype(F32) + m * vec[2:3, cols]
         X[pl.ds(mo(src * 64 + 32 * (y // 4) + 16 * s, 16), 16), cols] = m.astype(BF)
-        for n in range(4):
-            fy_copy(n, s).start()
+        for d in NEAR[1:]:
+            fy_copy(d, s).start()
         onward(0, s)
 
     def from_y(i, s):
         yy = (y + i) % YS
         b0 = blk(x, core, yy, s)
         rcopy(b0, b0, fys.at[s, yy], fyr.at[s, yy], {"tp": xl * YS + yy}).wait_recv()
-        if i in (2, 6):
-            fy_copy(4 if i == 6 else 5, s).start()
-            if i == (6 if s == 0 else 2):
-                fy_copy(6, s).start()
         onward(i, s)
 
     def from_x(i, s):
@@ -539,45 +533,56 @@
         for s in (0, 1):
             for i in NEAR:
                 fs_in(j, i, s).wait_recv()
-        gained(froms[j], 1 - core)
 
     mid(0)
+    hop(0, 2)
+    unpack(1)
+    mid(1)
     hop(1, 2)
-    mid(1)
-    for i in NEAR[1:]:
-        from_y(i, 0)
+
+    def from_q(i, s):
+        fq_in(i, s).wait_recv()
+        fs_copy(3, i, s).start()
+
+    idle = {1: (unpack, 7), 2: (unpack, 2), 3: (unpack, 6), 4: (unpack_sib, 1), 5: (unpack_sib, 7)}
+    for n in range(1, 8):
+        from_y(NEAR[n], 0)
+        if n in idle:
+            idle[n][0](idle[n][1])
     from_x(0, 0)
     hop(0, 3)
-    unpack(2)
-    unpack(6)
     for i in NEAR[1:]:
         from_y(i, 1)
         from_x(i, 0)
-    gained(x, core)
+    hop(1, 3)
+    for n in range(8):
+        from_x(NEAR[n], 1)
+        if n == 1:
+            unpack_sib(2)
+            unpack_sib(6)
+        if n == 3:
+            unpack(3)
+        if n == 5:
+            unpack(5)
     for i in NEAR:
-        from_x(i, 1)
-    hop(1, 3)
-    gained(xm, core)
-    gained(xp, core)
-    for s in (0, 1):
-        for i in NEAR:
-            fq_in(i, s).wait_recv()
-            fs_copy(3, i, s).start()
-    gained(xo, core)
-    unpack(3)
-    unpack(5)
-    unpack_sib(1)
-    unpack_sib(7)
-    unpack_sib(2)
-    unpack_sib(6)
-    for j in (0, 1, 2):
-        from_sib(j)
+        from_q(i, 0)
+    gained((xm, core), (xp, core))
+    for n in range(8):
+        from_q(NEAR[n], 1)
+        if n == 1:
+            from_sib(0)
+            gained((x, core), (x, 1 - core))
+        if n == 4:
+            unpack_sib(3)
+            unpack_sib(5)
+    from_sib(1)
+    from_sib(2)
+    gained((xm, 1 - core), (xp, 1 - core))
     hop(0, 4)
     hop(1, 4)
     unpack(4)
-    unpack_sib(3)
-    unpack_sib(5)
     from_sib(3)
+    gained((xo, core), (xo, 1 - core))
     gsc[...] = jnp.zeros((8, 1024), F32)
     gsc[0:1, :800] = gscale[...][None, :]
     gsc[1:2, :800] = uscale[...][None, :]
@@ -724,8 +729,8 @@
         for s in (0, 1):
             r_copy(d, s).wait_send()
     for s in (0, 1):
-        for n in range(7):
-            fy_copy(n, s).wait_send()
+        for d in NEAR[1:]:
+            fy_copy(d, s).wait_send()
         for i in range(YS):
             fx_copy(0, i, s).wait_send()
             fx_copy(1, i, s).wait_send()

time: 94.7 us -> 88.4 us (0.933)
  Pallas kernels: 93.1 us -> 86.6 us
    pallas_call x1, Pallas kernels: 93.1 us -> 86.6 us  [local(): pl.pallas_call(kernel, out_shape=jax.ShapeDtypeStruct((ROWS, 320), BF), i...]
where the time goes in v4:
time: 88.4 us; the launch traced here: 88 us
  Pallas kernels  86.6 us (98%)
  local copies, waits for them, and re-layouts  1.42 us (2%)
    pallas_call x1, Pallas kernels, local(): pl.pallas_call(kernel, out_shape=jax.ShapeDtypeStruct((ROWS, 320), BF), i...  86.6 us

profile of v4, /device:TPU:6, one launch (start us, length us, event | category | flops | bytes accessed | tf_op | source)
XLA Modules:
  0.0 88.0 jit_solution(18576652875764934)
XLA Ops:
  0.0 86.6 %layer.1 = bf16[64,320]{1,0:T(8,128)(2,1)} custom-call(bf16[64,5120]{1,0:T(8,128)(2,1)} %hid_hbm.1, f32[5120]{0:T(1024)} %again_hbm.1, s32[320,1280]{1,0:T(8,128)} %bitcast.2, f32[320]{0:T(512)} %qscale_hbm.1, f32[128]{0:T(128)} %qgain_hbm.1, f32[128]{0:T(128)} %kgain_hbm.1, bf16[1,4,128,512]{3,2,1,0:T(8,128)(2,1)} %kc_hbm.1, ...), custom_call_target="tpu_custom_call" | custom-call | tf_op jit(solution)/shard_map/layer/pallas_call | solution.py:791
  86.6 1.4 %copy.20 = bf16[64,320]{1,0:T(8,128)(2,1)} copy(bf16[64,320]{1,0:T(8,128)(2,1)} %layer.1) | data formatting | bytes 81920

commit v5 on v4

--- a/solution.py
+++ b/solution.py
@@ -110,6 +110,7 @@
     for to in (across, ZP, ZM):
         pl.semaphore_signal(barrier, inc=1, device_id=to, device_id_type=MESH)
 
+    p512[...] = one_hot(512, 128, 128)
     for c in loads:
         c.wait()
     turned = jnp.transpose(wdown[...])
@@ -121,7 +122,6 @@
         dn4[s, 0:40, 160:176] = piece[:, 384:400]
     gub[0, pl.ds(mo(src * 40, 8), 40), :] = gu4[src]
     dnp[src] = dn4[src]
-    p512[...] = one_hot(512, 128, 128)
     vec[0:1, :] = again[...][None, :]
     vec[1:2, :] = mgain[...][None, :]
     vec[2:3, :] = oscale[...][None, :]
@@ -416,6 +416,7 @@
     wo_share.wait_recv()
     unpack_wo(wo_r, (1 - xl) * 256)
 
+    hop(1, 1)
     lax.fori_loop(1, 16, wait_h, 0)
     got = hrecv[...]
     zcat = [dot(dot(picks[hl], got).astype(BF), p128[...]).astype(BF) for hl in range(4)]
@@ -443,7 +444,7 @@
         a, b = part(y, s)
         rs[s, y] = pm[a, b]
     unpack_sib(0)
-    hop(1, 1)
+    hop(0, 2)
 
     def blk(xx, cc, yy, s):
         r0 = ((xx // 2) * 2 + cc) * 64 + 32 * (yy // 4) + 16 * s
@@ -464,6 +465,9 @@
         return rcopy(b0, b0, fxs.at[s, way, i], fxr.at[s, way, i], MINUS if way == 0 else PLUS)
 
     def fq_copy(i, s):
+        if s == 1 and i in (5, 4):
+            b0 = blk(x, core, (y + i) % YS, s)
+            return rcopy(b0, b0, fqs.at[s, i], fqr.at[s, i], at_x(xo, core))
         way = i % 2
         b0 = blk(xm if way == 0 else xp, core, (y + i) % YS, s)
         return rcopy(b0, b0, fqs.at[s, i], fqr.at[s, i], PLUS if way == 0 else MINUS)
@@ -501,6 +505,8 @@
     def onward(i, s):
         fx_copy(0, i, s).start()
         fx_copy(1, i, s).start()
+        if s == 1 and i in (5, 4):
+            fq_copy(i, s).start()
         fs_copy(0, i, s).start()
 
     def mid(s):
@@ -525,7 +531,8 @@
     def from_x(i, s):
         fx_in(0, i, s).wait_recv()
         fx_in(1, i, s).wait_recv()
-        fq_copy(i, s).start()
+        if not (s == 1 and i in (5, 4)):
+            fq_copy(i, s).start()
         fs_copy(1, i, s).start()
         fs_copy(2, i, s).start()
 
@@ -535,7 +542,6 @@
                 fs_in(j, i, s).wait_recv()
 
     mid(0)
-    hop(0, 2)
     unpack(1)
     mid(1)
     hop(1, 2)
@@ -550,10 +556,11 @@
         if n in idle:
             idle[n][0](idle[n][1])
     from_x(0, 0)
-    hop(0, 3)
-    for i in NEAR[1:]:
-        from_y(i, 1)
-        from_x(i, 0)
+    for n in range(1, 8):
+        from_y(NEAR[n], 1)
+        from_x(NEAR[n], 0)
+        if n == 3:
+            hop(0, 3)
     hop(1, 3)
     for n in range(8):
         from_x(NEAR[n], 1)

time: 88.4 us -> 89.5 us (1.012); the launches traced: 88 us -> 87.9 us
  no operation moved by 1% of the time
where the time goes in v5:
time: 89.5 us; the launch traced here: 87.9 us
  Pallas kernels  86.4 us (97%)
  local copies, waits for them, and re-layouts  1.42 us (2%)
    pallas_call x1, Pallas kernels, local(): pl.pallas_call(kernel, out_shape=jax.ShapeDtypeStruct((ROWS, 320), BF), i...  86.4 us

profile of v5, /device:TPU:6, one launch (start us, length us, event | category | flops | bytes accessed | tf_op | source)
XLA Modules:
  0.0 87.9 jit_solution(6764969036452469457)
XLA Ops:
  0.0 86.4 %layer.1 = bf16[64,320]{1,0:T(8,128)(2,1)} custom-call(bf16[64,5120]{1,0:T(8,128)(2,1)} %hid_hbm.1, f32[5120]{0:T(1024)} %again_hbm.1, s32[320,1280]{1,0:T(8,128)} %bitcast.2, f32[320]{0:T(512)} %qscale_hbm.1, f32[128]{0:T(128)} %qgain_hbm.1, f32[128]{0:T(128)} %kgain_hbm.1, bf16[1,4,128,512]{3,2,1,0:T(8,128)(2,1)} %kc_hbm.1, ...), custom_call_target="tpu_custom_call" | custom-call | tf_op jit(solution)/shard_map/layer/pallas_call | solution.py:798
  86.4 1.4 %copy.20 = bf16[64,320]{1,0:T(8,128)(2,1)} copy(bf16[64,320]{1,0:T(8,128)(2,1)} %layer.1) | data formatting | bytes 81920

commit v6 on v4

--- a/solution.py
+++ b/solution.py
@@ -110,6 +110,7 @@
     for to in (across, ZP, ZM):
         pl.semaphore_signal(barrier, inc=1, device_id=to, device_id_type=MESH)
 
+    p512[...] = one_hot(512, 128, 128)
     for c in loads:
         c.wait()
     turned = jnp.transpose(wdown[...])
@@ -121,7 +122,6 @@
         dn4[s, 0:40, 160:176] = piece[:, 384:400]
     gub[0, pl.ds(mo(src * 40, 8), 40), :] = gu4[src]
     dnp[src] = dn4[src]
-    p512[...] = one_hot(512, 128, 128)
     vec[0:1, :] = again[...][None, :]
     vec[1:2, :] = mgain[...][None, :]
     vec[2:3, :] = oscale[...][None, :]
@@ -464,6 +464,9 @@
         return rcopy(b0, b0, fxs.at[s, way, i], fxr.at[s, way, i], MINUS if way == 0 else PLUS)
 
     def fq_copy(i, s):
+        if s == 1 and i in (5, 4):
+            b0 = blk(x, core, (y + i) % YS, s)
+            return rcopy(b0, b0, fqs.at[s, i], fqr.at[s, i], at_x(xo, core))
         way = i % 2
         b0 = blk(xm if way == 0 else xp, core, (y + i) % YS, s)
         return rcopy(b0, b0, fqs.at[s, i], fqr.at[s, i], PLUS if way == 0 else MINUS)
@@ -501,6 +504,8 @@
     def onward(i, s):
         fx_copy(0, i, s).start()
         fx_copy(1, i, s).start()
+        if s == 1 and i in (5, 4):
+            fq_copy(i, s).start()
         fs_copy(0, i, s).start()
 
     def mid(s):
@@ -525,7 +530,8 @@
     def from_x(i, s):
         fx_in(0, i, s).wait_recv()
         fx_in(1, i, s).wait_recv()
-        fq_copy(i, s).start()
+        if not (s == 1 and i in (5, 4)):
+            fq_copy(i, s).start()
         fs_copy(1, i, s).start()
         fs_copy(2, i, s).start()
 

time: 88.4 us -> 88.1 us (level)
  Pallas kernels: 86.6 us -> 85.6 us
    pallas_call x1, Pallas kernels: 86.6 us -> 85.6 us  [local(): pl.pallas_call(kernel, out_shape=jax.ShapeDtypeStruct((ROWS, 320), BF), i...]
where the time goes in v6:
time: 88.1 us; the launch traced here: 87 us
  Pallas kernels  85.6 us (97%)
  local copies, waits for them, and re-layouts  1.42 us (2%)
    pallas_call x1, Pallas kernels, local(): pl.pallas_call(kernel, out_shape=jax.ShapeDtypeStruct((ROWS, 320), BF), i...  85.6 us

profile of v6, /device:TPU:6, one launch (start us, length us, event | category | flops | bytes accessed | tf_op | source)
XLA Modules:
  0.0 87.0 jit_solution(17821204479961824962)
XLA Ops:
  0.0 85.6 %layer.1 = bf16[64,320]{1,0:T(8,128)(2,1)} custom-call(bf16[64,5120]{1,0:T(8,128)(2,1)} %hid_hbm.1, f32[5120]{0:T(1024)} %again_hbm.1, s32[320,1280]{1,0:T(8,128)} %bitcast.2, f32[320]{0:T(512)} %qscale_hbm.1, f32[128]{0:T(128)} %qgain_hbm.1, f32[128]{0:T(128)} %kgain_hbm.1, bf16[1,4,128,512]{3,2,1,0:T(8,128)(2,1)} %kc_hbm.1, ...), custom_call_target="tpu_custom_call" | custom-call | tf_op jit(solution)/shard_map/layer/pallas_call | solution.py:797
  85.6 1.4 %copy.20 = bf16[64,320]{1,0:T(8,128)(2,1)} copy(bf16[64,320]{1,0:T(8,128)(2,1)} %layer.1) | data formatting | bytes 81920
